TPU v7x, 8 devices: a whole 2x2x1 slice. The times are simulated.
8 devices in a mesh: dp: 1 (over z), tp: 8 (over y, x, core).
Axes of the slice: x: 2, y: 2, z: 1, core: 2. Of those that a mesh axis runs over, the one named last changes fastest.
Arguments:
- hidden: bfloat16 [32, 1536], P('dp')
- lengths: int32 [32], P('dp')
- choice: int32 [2, 32, 8], P(None, 'dp')
- keys_one: bfloat16 [32, 128, 8, 64], P('dp', 'tp')
- vals_one: bfloat16 [32, 128, 8, 64], P('dp', 'tp')
- keys_two: bfloat16 [32, 128, 8, 64], P('dp', 'tp')
- vals_two: bfloat16 [32, 128, 8, 64], P('dp', 'tp')
- g_attn: bfloat16 [2, 1536], replicated
- w_q: bfloat16 [2, 1536, 1536], P(None, None, 'tp')
- w_k: bfloat16 [2, 1536, 512], P(None, None, 'tp')
- w_v: bfloat16 [2, 1536, 512], P(None, None, 'tp')
- w_o: bfloat16 [2, 1536, 1536], P(None, 'tp')
- g_mlp: bfloat16 [2, 1536], replicated
- w_router: bfloat16 [2, 1536, 40], replicated
- w_gate: bfloat16 [2, 40, 1536, 512], P(None, None, None, 'tp')
- w_up: bfloat16 [2, 40, 1536, 512], P(None, None, None, 'tp')
- w_down: bfloat16 [2, 40, 512, 1536], P(None, None, 'tp')
Outputs:
- output 1: bfloat16 [32, 1536], P('dp')
- output 2: bfloat16 [32, 128, 8, 64], P('dp', None, 'tp')
- output 3: bfloat16 [32, 128, 8, 64], P('dp', None, 'tp')
- output 4: bfloat16 [32, 128, 8, 64], P('dp', None, 'tp')
- output 5: bfloat16 [32, 128, 8, 64], P('dp', None, 'tp')
All inputs are finite; a program needn't handle non-finite values.
Results may differ from a plain program's by a relative error of at most 0.02.
Values are sent between devices in bfloat16 or wider.
A program may use at most 1 GiB of HBM per device.

v0:
```python
import jax
import jax.numpy as jnp
from jax import lax
from jax.sharding import PartitionSpec as P

EPS = 1e-5
THETA = 1000000.0


def rms_norm(tensor, gain_vec):
    tensor_f = tensor.astype(jnp.float32)
    scale = lax.rsqrt(jnp.mean(tensor_f * tensor_f, axis=-1, keepdims=True) + EPS)
    return (tensor_f * scale * gain_vec.astype(jnp.float32)).astype(jnp.bfloat16)


def apply_rope(tensor, lengths):
    head_dim = tensor.shape[-1]
    half_dim = head_dim // 2
    inv_freq = THETA ** (-2.0 * jnp.arange(half_dim, dtype=jnp.float32) / head_dim)
    angle = lengths.astype(jnp.float32)[:, None] * inv_freq[None, :]
    cos_part = jnp.cos(angle)[:, None, :]
    sin_part = jnp.sin(angle)[:, None, :]
    lower_half = tensor[..., :half_dim]
    upper_half = tensor[..., half_dim:]
    return jnp.concatenate([lower_half * cos_part - upper_half * sin_part, upper_half * cos_part + lower_half * sin_part], axis=-1)


def expert_block(x_mid, choice, g_mlp, w_router, w_gate, w_up, w_down):
    normed = rms_norm(x_mid, g_mlp)
    logits = jnp.dot(normed, w_router, preferred_element_type=jnp.float32)
    onehot = (choice[:, :, None] == jnp.arange(w_router.shape[1])[None, None, :]).astype(jnp.float32)
    gate_prob = jax.nn.softmax(jnp.sum(onehot * logits[:, None, :], axis=-1), axis=-1)
    gate_mat = jnp.sum(gate_prob[:, :, None] * onehot, axis=1)
    gate_act = jnp.einsum('bd,edf->bef', normed, w_gate, preferred_element_type=jnp.float32)
    up_act = jnp.einsum('bd,edf->bef', normed, w_up, preferred_element_type=jnp.float32)
    expert_in = (jax.nn.silu(gate_act) * up_act * gate_mat[:, :, None]).astype(jnp.bfloat16)
    return jnp.einsum('bef,efd->bd', expert_in, w_down, preferred_element_type=jnp.float32)


def decode_layer(hidden, lengths, choice, key_cache, val_cache, g_attn, w_q, w_k, w_v, w_o, g_mlp, w_router, w_gate, w_up, w_down):
    batch_rows, seq_len, kv_heads, head_dim = key_cache.shape
    num_heads = w_q.shape[1] // head_dim
    normed = rms_norm(hidden, g_attn)
    query_rot = apply_rope(jnp.dot(normed, w_q, preferred_element_type=jnp.float32).reshape(batch_rows, num_heads, head_dim), lengths).astype(jnp.bfloat16)
    key_new = apply_rope(jnp.dot(normed, w_k, preferred_element_type=jnp.float32).reshape(batch_rows, kv_heads, head_dim), lengths).astype(jnp.bfloat16)
    val_new = jnp.dot(normed, w_v, preferred_element_type=jnp.float32).astype(jnp.bfloat16).reshape(batch_rows, kv_heads, head_dim)
    positions = jnp.arange(seq_len)
    is_new = (positions[None, :] == lengths[:, None])[:, :, None, None]
    key_cache = jnp.where(is_new, key_new[:, None], key_cache)
    val_cache = jnp.where(is_new, val_new[:, None], val_cache)
    query_grp = query_rot.reshape(batch_rows, kv_heads, num_heads // kv_heads, head_dim)
    scores = jnp.einsum('bgrd,bsgd->bgrs', query_grp, key_cache, preferred_element_type=jnp.float32) * head_dim ** -0.5
    is_valid = (positions[None, :] <= lengths[:, None])[:, None, None, :]
    attn_prob = jax.nn.softmax(jnp.where(is_valid, scores, -1e30), axis=-1).astype(jnp.bfloat16)
    attn_vec = jnp.einsum('bgrs,bsgd->bgrd', attn_prob, val_cache, preferred_element_type=jnp.float32).astype(jnp.bfloat16).reshape(batch_rows, num_heads * head_dim)
    attn_sum = lax.psum(jnp.dot(attn_vec, w_o, preferred_element_type=jnp.float32).astype(jnp.bfloat16), 'tp')
    x_mid = (hidden.astype(jnp.float32) + attn_sum.astype(jnp.float32)).astype(jnp.bfloat16)
    moe_sum = lax.psum(expert_block(x_mid, choice, g_mlp, w_router, w_gate, w_up, w_down).astype(jnp.bfloat16), 'tp')
    return (x_mid.astype(jnp.float32) + moe_sum.astype(jnp.float32)).astype(jnp.bfloat16), key_cache, val_cache


def solution(mesh):
    seq_spec = P('dp', 'tp', None, None)
    head_spec = P('dp', None, 'tp', None)
    col_spec = P(None, None, 'tp')
    ff_spec = P(None, None, None, 'tp')

    def local_step(hidden, lengths, choice, keys_one, vals_one, keys_two, vals_two, g_attn, w_q, w_k, w_v, w_o, g_mlp, w_router, w_gate, w_up, w_down):
        moved = [lax.all_to_all(cache_blk, 'tp', 2, 1, tiled=True) for cache_blk in (keys_one, vals_one, keys_two, vals_two)]
        results = []
        for layer_idx in range(2):
            hidden, key_cache, val_cache = decode_layer(hidden, lengths, choice[layer_idx], moved[2 * layer_idx], moved[2 * layer_idx + 1], g_attn[layer_idx], w_q[layer_idx], w_k[layer_idx], w_v[layer_idx], w_o[layer_idx], g_mlp[layer_idx], w_router[layer_idx], w_gate[layer_idx], w_up[layer_idx], w_down[layer_idx])
            results.append(key_cache)
            results.append(val_cache)
        return (hidden, results[0], results[1], results[2], results[3])

    return jax.shard_map(local_step, mesh=mesh, in_specs=(P('dp', None), P('dp'), P(None, 'dp', None), seq_spec, seq_spec, seq_spec, seq_spec, P(), col_spec, col_spec, col_spec, P(None, 'tp', None), P(), P(), ff_spec, ff_spec, P(None, None, 'tp', None)), out_specs=(P('dp', None), head_spec, head_spec, head_spec, head_spec), check_vma=False)
```

profile of v0, /device:TPU:0, one launch (start us, length us, event | category | flops | bytes accessed | tf_op | source)
XLA Modules:
  0.0 286.9 jit_solution(2085682192473477183)
XLA Ops:
  7.2 1.5 copy.152
  8.7 1.5 reshape.468
  10.2 4.3 %all-to-all-start.1 = ((bf16[8,2,16384]{2,1,0:T(2,128)(2,1)}), bf16[8,2,16384]{2,1,0:T(2,128)(2,1)S(1)}, u32[]{:S(2)}, u32[]{:S(2)}) async-start(bf16[8,2,16384]{2,1,0:T(2,128)(2,1)} %reshape.468), calls=%async_computation.1 | async-start | bytes 1048576 | tf_op jit(solution)/shard_map/all_to_all | solution.py:69
  14.5 1.4 copy.150
  15.9 1.5 reshape.466
  17.6 1.4 copy.153
  18.9 1.5 reshape.470
  20.6 1.1 convolution_bitcast_fusion.1
  21.9 0.9 fusion.157
  22.8 0.4 fusion.118
  23.3 1.4 copy.151
  24.6 1.5 reshape.472
  26.5 0.2 convolution_convert_fusion.5
  26.7 2.9 %all-to-all-start = ((bf16[8,2,16384]{2,1,0:T(2,128)(2,1)}), bf16[8,2,16384]{2,1,0:T(2,128)(2,1)S(1)}, u32[]{:S(2)}, u32[]{:S(2)}) async-start(bf16[8,2,16384]{2,1,0:T(2,128)(2,1)} %reshape.470), calls=%async_computation | async-start | bytes 1048576 | tf_op jit(solution)/shard_map/all_to_all | solution.py:69
  29.7 0.7 reshape.469
  30.4 0.2 bitcast_bitcast_fusion.2
  30.6 8.7 %all-to-all-done = bf16[8,2,16384]{2,1,0:T(2,128)(2,1)S(1)} async-done(((bf16[8,2,16384]{2,1,0:T(2,128)(2,1)}), bf16[8,2,16384]{2,1,0:T(2,128)(2,1)S(1)}, u32[]{:S(2)}, u32[]{:S(2)}) %all-to-all-start) | async-done | bytes 524320 | tf_op jit(solution)/shard_map/all_to_all | solution.py:69
  39.3 2.9 %all-to-all-start.3 = ((bf16[8,2,16384]{2,1,0:T(2,128)(2,1)}), bf16[8,2,16384]{2,1,0:T(2,128)(2,1)}, u32[]{:S(2)}, u32[]{:S(2)}) async-start(bf16[8,2,16384]{2,1,0:T(2,128)(2,1)} %reshape.466), calls=%async_computation.3 | async-start | bytes 1048576 | tf_op jit(solution)/shard_map/all_to_all | solution.py:69
  42.2 0.7 reshape.471
  43.0 0.3 copy.105
  43.3 0.9 fusion.55
  44.2 0.3 copy.109
  44.6 0.2 fusion.158
  44.8 1.1 convolution_convert_fusion.3
  46.0 5.7 %all-to-all-done.3 = bf16[8,2,16384]{2,1,0:T(2,128)(2,1)} async-done(((bf16[8,2,16384]{2,1,0:T(2,128)(2,1)}), bf16[8,2,16384]{2,1,0:T(2,128)(2,1)}, u32[]{:S(2)}, u32[]{:S(2)}) %all-to-all-start.3) | async-done | bytes 524320 | tf_op jit(solution)/shard_map/all_to_all | solution.py:69
  51.7 2.9 %all-to-all-start.2 = ((bf16[8,2,16384]{2,1,0:T(2,128)(2,1)}), bf16[8,2,16384]{2,1,0:T(2,128)(2,1)}, u32[]{:S(2)}, u32[]{:S(2)}) async-start(bf16[8,2,16384]{2,1,0:T(2,128)(2,1)} %reshape.472), calls=%async_computation.2 | async-start | bytes 1048576 | tf_op jit(solution)/shard_map/all_to_all | solution.py:69
  54.6 1.9 convolution_convert_fusion.1
  56.6 0.2 all-reduce.7.cloned.1.call-start
  56.8 2.3 reshape.467
  59.3 4.8 %all-to-all-done.2 = bf16[8,2,16384]{2,1,0:T(2,128)(2,1)} async-done(((bf16[8,2,16384]{2,1,0:T(2,128)(2,1)}), bf16[8,2,16384]{2,1,0:T(2,128)(2,1)}, u32[]{:S(2)}, u32[]{:S(2)}) %all-to-all-start.2) | async-done | bytes 524320 | tf_op jit(solution)/shard_map/all_to_all | solution.py:69
  64.1 2.3 reshape.473
  66.4 36.1 %all-reduce.5.cloned.1.call-done = bf16[32,1536]{1,0:T(8,128)(2,1)} async-done(((bf16[32,1536]{1,0:T(8,128)(2,1)}), bf16[32,1536]{1,0:T(8,128)(2,1)}) %all-reduce.5.cloned.1.call-update) | async-done | bytes 98320 | tf_op jit(solution)/shard_map/psum | solution.py:56
  102.5 1.0 fusion.84
  103.5 1.0 fusion.86
  104.5 7.7 %fusion.12 = f32[32,40,64]{2,0,1:T(8,128)} fusion(bf16[2,40,1536,64]{2,3,1,0:T(8,128)(2,1)} %param.31, bf16[32,1536]{1,0:T(8,128)(2,1)S(1)} %fusion.86), kind=kOutput, calls=%fused_computation.12 | convolution fusion | flops 251658240 | bytes 8290304 | tf_op jit(solution)/shard_map/bd,edf->bef/dot_general | solution.py:34
  112.3 1.0 fusion.106
  113.3 0.2 select_reduce_fusion.3
  114.0 9.3 %fusion.29 = bf16[32,1536]{1,0:T(8,128)(2,1)} fusion(bf16[2,40,64,1536]{3,2,1,0:T(8,128)(2,1)} %param.33, bf16[2,40,1536,64]{2,3,1,0:T(8,128)(2,1)} %param.32, f32[32,40,64]{2,0,1:T(8,128)} %fusion.12, f32[32,40]{0,1:T(8,128)S(1)} %copy.115, bf16[32,1536]{1,0:T(8,128)(2,1)S(1)} %fusion.86), kind=kOutput, calls=%fused_computation.23 | convolution fusion | flops 503939072 | bytes 16585728 | tf_op jit(solution)/shard_map/bef,efd->bd/dot_general | solution.py:37
  123.6 0.3 copy.121
  123.9 0.3 copy.117
  124.2 40.8 %all-reduce.7.cloned.1.call-done = bf16[32,1536]{1,0:T(8,128)(2,1)} async-done(((bf16[32,1536]{1,0:T(8,128)(2,1)}), bf16[32,1536]{1,0:T(8,128)(2,1)}) %all-reduce.7.cloned.1.call-update) | async-done | bytes 98320 | tf_op jit(solution)/shard_map/psum | solution.py:58
  165.0 1.0 fusion.88
  166.0 1.2 convolution_convert_fusion.4
  167.2 1.2 convolution_bitcast_fusion
  168.5 1.4 fusion.113
  170.2 0.9 fusion.54
  171.2 0.2 fusion.159
  171.4 1.1 convolution_convert_fusion.2
  172.6 1.9 convolution_convert_fusion
  174.6 0.3 all-reduce.11.cloned.1.call-start
  174.9 41.3 %all-reduce.9.cloned.1.call-done = bf16[32,1536]{1,0:T(8,128)(2,1)} async-done(((bf16[32,1536]{1,0:T(8,128)(2,1)}), bf16[32,1536]{1,0:T(8,128)(2,1)}) %all-reduce.9.cloned.1.call-update) | async-done | bytes 98320 | tf_op jit(solution)/shard_map/psum | solution.py:56
  216.2 1.0 fusion.92
  217.3 1.0 fusion.94
  218.3 7.7 %fusion.6 = f32[32,40,64]{2,0,1:T(8,128)} fusion(bf16[2,40,1536,64]{2,3,1,0:T(8,128)(2,1)} %param.31, bf16[32,1536]{1,0:T(8,128)(2,1)S(1)} %fusion.94), kind=kOutput, calls=%fused_computation.6 | convolution fusion | flops 251658240 | bytes 8290304 | tf_op jit(solution)/shard_map/bd,edf->bef/dot_general | solution.py:34
  226.0 1.0 fusion.104
  227.0 0.2 select_reduce_fusion.1
  227.8 9.3 %fusion.26 = bf16[32,1536]{1,0:T(8,128)(2,1)} fusion(bf16[2,40,64,1536]{3,2,1,0:T(8,128)(2,1)} %param.33, bf16[2,40,1536,64]{2,3,1,0:T(8,128)(2,1)} %param.32, f32[32,40,64]{2,0,1:T(8,128)} %fusion.6, f32[32,40]{0,1:T(8,128)S(1)} %copy.127, bf16[32,1536]{1,0:T(8,128)(2,1)S(1)} %fusion.94), kind=kOutput, calls=%fused_computation.22 | convolution fusion | flops 503939072 | bytes 16585728 | tf_op jit(solution)/shard_map/bef,efd->bd/dot_general | solution.py:37
  237.1 5.1 %bitcast_select_fusion = (bf16[32,128,1,64]{3,1,0,2:T(8,128)(2,1)}, bf16[32,128,1,64]{3,1,0,2:T(8,128)(2,1)}, bf16[32,128,1,64]{3,1,0,2:T(8,128)(2,1)}, bf16[32,128,1,64]{3,1,0,2:T(8,128)(2,1)}) fusion(bf16[32,8,16,1,64]{4,2,1,0,3:T(8,128)(2,1)S(1)} %copy.121, pred[32,128]{1,0:T(8,128)(4,1)S(1)} %get-tuple-element.50, ...), kind=kLoop, calls=%fused_computation.46 | loop fusion | flops 1048576 | bytes 4214784 | tf_op jit(solution)/shard_map/jit(_where)/select_n | solution.py:50
  242.3 2.3 copy.132
  244.6 2.3 copy.133
  246.9 2.3 copy.134
  249.3 2.3 copy.135
  251.6 27.1 %all-reduce.11.cloned.1.call-done = bf16[32,1536]{1,0:T(8,128)(2,1)} async-done(((bf16[32,1536]{1,0:T(8,128)(2,1)}), bf16[32,1536]{1,0:T(8,128)(2,1)}) %all-reduce.11.cloned.1.call-update) | async-done | bytes 98320 | tf_op jit(solution)/shard_map/psum | solution.py:58
  278.8 1.6 fusion.95
  (72 shorter events, 3.5 us)
Async XLA Ops:
  7.2 10.2 %copy-start.7 = (bf16[2,1536]{1,0:T(2,128)(2,1)S(1)}, bf16[2,1536]{1,0:T(2,128)(2,1)}, u32[]{:S(2)}) copy-start(bf16[2,1536]{1,0:T(2,128)(2,1)} %param.24) | copy-start | bytes 18436
  7.2 10.2 %copy-start.3 = (bf16[32,1536]{1,0:T(8,128)(2,1)S(1)}, bf16[32,1536]{1,0:T(8,128)(2,1)}, u32[]{:S(2)}) copy-start(bf16[32,1536]{1,0:T(8,128)(2,1)} %param.17) | copy-start | bytes 294916
  7.2 13.3 %copy-start.10 = (s32[32]{0:T(128)S(1)}, s32[32]{0:T(128)}, u32[]{:S(2)}) copy-start(s32[32]{0:T(128)} %param.18) | copy-start | bytes 388
  7.2 14.7 %copy-start.4 = (bf16[2,1536,192]{1,2,0:T(8,128)(2,1)S(1)}, bf16[2,1536,192]{1,2,0:T(8,128)(2,1)}, u32[]{:S(2)}) copy-start(bf16[2,1536,192]{1,2,0:T(8,128)(2,1)} %param.25) | copy-start | bytes 3538948
  7.2 16.0 %copy-start.9 = (s32[2,32,8]{1,2,0:T(8,128)S(1)}, s32[2,32,8]{1,2,0:T(8,128)}, u32[]{:S(2)}) copy-start(s32[2,32,8]{1,2,0:T(8,128)} %param.19) | copy-start | bytes 6148
  10.2 16.2 %copy-start.8 = (bf16[2,1536]{1,0:T(2,128)(2,1)S(1)}, bf16[2,1536]{1,0:T(2,128)(2,1)}, u32[]{:S(2)}) copy-start(bf16[2,1536]{1,0:T(2,128)(2,1)} %param.29) | copy-start | bytes 18436
  10.2 16.3 %copy-start.11 = (bf16[2,1536,64]{1,2,0:T(8,128)(2,1)S(1)}, bf16[2,1536,64]{1,2,0:T(8,128)(2,1)}, u32[]{:S(2)}) copy-start(bf16[2,1536,64]{1,2,0:T(8,128)(2,1)} %param.27) | copy-start | bytes 1179652
  10.2 16.5 %all-to-all-start.1 = ((bf16[8,2,16384]{2,1,0:T(2,128)(2,1)}), bf16[8,2,16384]{2,1,0:T(2,128)(2,1)S(1)}, u32[]{:S(2)}, u32[]{:S(2)}) async-start(bf16[8,2,16384]{2,1,0:T(2,128)(2,1)} %reshape.468), calls=%async_computation.1 | async-start | bytes 1048576 | tf_op jit(solution)/shard_map/all_to_all | solution.py:69
  26.7 12.6 %all-to-all-start = ((bf16[8,2,16384]{2,1,0:T(2,128)(2,1)}), bf16[8,2,16384]{2,1,0:T(2,128)(2,1)S(1)}, u32[]{:S(2)}, u32[]{:S(2)}) async-start(bf16[8,2,16384]{2,1,0:T(2,128)(2,1)} %reshape.470), calls=%async_computation | async-start | bytes 1048576 | tf_op jit(solution)/shard_map/all_to_all | solution.py:69
  39.3 12.4 %all-to-all-start.3 = ((bf16[8,2,16384]{2,1,0:T(2,128)(2,1)}), bf16[8,2,16384]{2,1,0:T(2,128)(2,1)}, u32[]{:S(2)}, u32[]{:S(2)}) async-start(bf16[8,2,16384]{2,1,0:T(2,128)(2,1)} %reshape.466), calls=%async_computation.3 | async-start | bytes 1048576 | tf_op jit(solution)/shard_map/all_to_all | solution.py:69
  44.5 12.1 %copy-start = (bf16[32,8,16,1,64]{4,2,1,0,3:T(8,128)(2,1)}, bf16[32,8,16,1,64]{4,2,1,0,3:T(8,128)(2,1)S(1)}, u32[]{:S(2)}) copy-start(bf16[32,8,16,1,64]{4,2,1,0,3:T(8,128)(2,1)S(1)} %copy.109) | copy-start | bytes 1572868
  51.7 12.4 %all-to-all-start.2 = ((bf16[8,2,16384]{2,1,0:T(2,128)(2,1)}), bf16[8,2,16384]{2,1,0:T(2,128)(2,1)}, u32[]{:S(2)}, u32[]{:S(2)}) async-start(bf16[8,2,16384]{2,1,0:T(2,128)(2,1)} %reshape.472), calls=%async_computation.2 | async-start | bytes 1048576 | tf_op jit(solution)/shard_map/all_to_all | solution.py:69
  54.6 47.9 %all-reduce.5.cloned.1.call-start = ((), (), s32[]{:S(2)}) async-start(), calls=%async_computation.4 | async-start | bytes 196608 | tf_op jit(solution)/shard_map/psum | solution.py:56
  56.6 108.4 %all-reduce.7.cloned.1.call-start = ((), (), s32[]{:S(2)}) async-start(), calls=%async_computation.5 | async-start | bytes 196608 | tf_op jit(solution)/shard_map/psum | solution.py:58
  114.0 50.9 %copy-start.6 = (bf16[32,1536]{1,0:T(8,128)(2,1)S(1)}, bf16[32,1536]{1,0:T(8,128)(2,1)}, u32[]{:S(2)}) copy-start(bf16[32,1536]{1,0:T(8,128)(2,1)} %all-reduce.5.cloned.1.call-done) | copy-start | bytes 294916
  123.3 92.9 %all-reduce.9.cloned.1.call-start = ((), (), s32[]{:S(2)}) async-start(), calls=%async_computation.6 | async-start | bytes 196608 | tf_op jit(solution)/shard_map/psum | solution.py:56
  124.2 101.8 %copy-start.2 = (bf16[32,8,16,1,64]{4,2,1,0,3:T(8,128)(2,1)}, bf16[32,8,16,1,64]{4,2,1,0,3:T(8,128)(2,1)S(1)}, u32[]{:S(2)}) copy-start(bf16[32,8,16,1,64]{4,2,1,0,3:T(8,128)(2,1)S(1)} %copy.117) | copy-start | bytes 1572868
  174.6 104.2 %all-reduce.11.cloned.1.call-start = ((), (), s32[]{:S(2)}) async-start(), calls=%async_computation.7 | async-start | bytes 196608 | tf_op jit(solution)/shard_map/psum | solution.py:58
  227.8 9.3 %copy-start.1 = (bf16[32,8,16,1,64]{4,2,1,0,3:T(8,128)(2,1)S(1)}, bf16[32,8,16,1,64]{4,2,1,0,3:T(8,128)(2,1)}, u32[]{:S(2)}) copy-start(bf16[32,8,16,1,64]{4,2,1,0,3:T(8,128)(2,1)} %copy-done) | copy-start | bytes 1572868
  237.1 41.7 %copy-start.5 = (bf16[32,1536]{1,0:T(8,128)(2,1)S(1)}, bf16[32,1536]{1,0:T(8,128)(2,1)}, u32[]{:S(2)}) copy-start(bf16[32,1536]{1,0:T(8,128)(2,1)} %all-reduce.9.cloned.1.call-done) | copy-start | bytes 294916
Sparse Core Ops, SparseCore 0:
  59.0 43.4 all-reduce.4
  123.5 41.4 all-reduce.6
  174.7 41.5 all-reduce.8
  237.2 41.4 all-reduce.10
where the time goes:
time: 288 us; the launch traced here: 287 us
  waiting for transfers between devices  165 us (57%)
  matrix products  49.6 us (17%)
  local copies, waits for them, and re-layouts  30.4 us (11%)
  other arithmetic  14.5 us (5%)
  between operations  14.2 us (5%)
  starting transfers between devices  13.6 us (5%)
    psum x2, waiting for transfers between devices, decode_layer(): lax.psum(jnp.dot(attn_vec, w_o, preferred_element_type=jnp.float32).astyp...  77.4 us
    psum x2, waiting for transfers between devices, decode_layer(): lax.psum(expert_block(x_mid, choice, g_mlp, w_router, w_gate, w_up, w_dow...  67.9 us
    unnamed x40, local copies, waits for them, and re-layouts  26.9 us
    all_to_all x4, waiting for transfers between devices, local_step(): lax.all_to_all(cache_blk, 'tp', 2, 1, tiled=True)  19.3 us
    dot_general x2, matrix products, expert_block(): jnp.einsum('bef,efd->bd', expert_in, w_down, preferred_element_type=jnp.f...  18.6 us
    dot_general x2, matrix products, expert_block(): jnp.einsum('bd,edf->bef', normed, w_gate, preferred_element_type=jnp.floa...  15.5 us
    all_to_all x4, starting transfers between devices, local_step(): lax.all_to_all(cache_blk, 'tp', 2, 1, tiled=True)  13 us
  transfers between devices with their start and end apart: 8, of which 7 were waited for; matrix products, arithmetic and copies ran while one was open for 14% of the time, Pallas kernels for 0%

commit v1 on v0

v1 whole, which is shorter than its diff:
```python
import jax
import jax.numpy as jnp
import numpy as np
from jax import lax
from jax.experimental import pallas as pl
from jax.experimental.pallas import tpu as pltpu
from jax.sharding import PartitionSpec as P

EPS = 1e-5
THETA = 1000000.0
N = 8
B = 32
D = 1536
SEQ = 128
CH = 4
QUADS = 10
NT = (((1,), (1,)), ((), ()))
PEERS = ((1, 1, 0), (1, 0, 1), (0, 1, 0), (1, 1, 1), (1, 0, 0), (0, 1, 1), (0, 0, 1))


def rope_tables():
    half = 32
    inv = np.power(np.float32(THETA), (-2.0 * np.arange(half, dtype=np.float32) / 64).astype(np.float32)).astype(np.float32)
    angle = (np.arange(SEQ, dtype=np.float32)[:, None] * inv[None, :]).astype(np.float32).astype(np.float64)
    cos = np.tile(np.cos(angle), (1, 4)).astype(np.float32)
    sin = np.tile(np.sin(angle), (1, 4)).astype(np.float32)
    return cos, sin


def dot_nt(a, b):
    return lax.dot_general(a, b, NT, preferred_element_type=jnp.float32)


def dot_nn(a, b):
    return jnp.dot(a, b, preferred_element_type=jnp.float32)


def kernel(len_s, hid_h, choice_h, k1_h, v1_h, k2_h, v2_h, ga_h, wq_h, wk_h, wv_h, wo_h, gm_h, wr_h, wg_h, wu_h, wd_h, cos_h, sin_h,
           hid_o, kv1_o, kv2_o,
           wg, wu, wd, wqkv, wo, wr, xk, xv, stage, send, recv, outs, hb, psend, rsb, m_s, qs, sc, os_, kvn, cos_t, sin_t, cos_b, sin_b, choice_v, ga, gm, mask_s, gx, act, acc,
           s_in, s_w, s_small, s_out, a2a_ss, a2a_rs, rs_ss, rs_rs, ag_ss, ag_rs):
    me = lax.axis_index('tp')
    my, mx, mc = me // 4, (me // 2) % 2, me % 2
    peers = []
    for dy, dx, dc in PEERS:
        peers.append(((my + dy) % 2) * 4 + ((mx + dx) % 2) * 2 + (mc + dc) % 2)

    def dev(t):
        return {'tp': t}

    barrier = pltpu.get_barrier_semaphore()
    for t in peers:
        pl.semaphore_signal(barrier, inc=1, device_id=dev(t), device_id_type=pl.DeviceIdType.MESH)

    caches = ((k1_h, v1_h), (k2_h, v2_h))
    cache_cp = {}
    for l in range(2):
        for c in range(CH):
            for i, buf in enumerate((xk, xv)):
                rows = pl.ds(c * 128, 128)
                cp = pltpu.make_async_copy(caches[l][i].at[rows], buf.at[l, rows], s_in.at[l, c, i])
                cache_cp[l, c, i] = cp

    small = [
        (cos_h, cos_t), (sin_h, sin_t), (choice_h, choice_v), (ga_h, ga), (gm_h, gm), (wr_h, wr), (wo_h, wo),
    ]
    for l in range(2):
        small.append((wq_h.at[l, pl.ds(0, 128)], wqkv.at[l, pl.ds(0, 128)]))
        small.append((wk_h.at[l], wqkv.at[l, pl.ds(128, 64)]))
        small.append((wq_h.at[l, pl.ds(128, 64)], wqkv.at[l, pl.ds(192, 64)]))
        small.append((wv_h.at[l], wqkv.at[l, pl.ds(320, 64)]))
    for j in range(N):
        small.append((hid_h.at[pl.ds(16 * (j // 4), 16), pl.ds(384 * (j % 4), 384)], hb.at[0, j]))
    small_cp = [pltpu.make_async_copy(src, dst, s_small.at[i]) for i, (src, dst) in enumerate(small)]

    for c in range(CH):
        cache_cp[0, c, 0].start()
        cache_cp[0, c, 1].start()
    for cp in small_cp:
        cp.start()
    for c in range(CH):
        cache_cp[1, c, 0].start()
        cache_cp[1, c, 1].start()

    def weight_copies(l, j):
        rows = pl.ds(pl.multiple_of(j * 256, 256), 256)
        return [pltpu.make_async_copy(src.at[l, rows], dst.at[l, rows], s_w.at[l, j, i])
                for i, (src, dst) in enumerate(((wg_h, wg), (wu_h, wu), (wd_h, wd)))]

    for l in range(2):
        def start_weights(j, _, l=l):
            for cp in weight_copies(l, j):
                cp.start()
            return 0
        lax.fori_loop(0, QUADS, start_weights, 0)

    def prep(l, c):
        cache_cp[l, c, 0].wait()
        cache_cp[l, c, 1].wait()
        for i in range(2):
            rows = pl.ds(c * 128 + i * 64, 64)
            kk = xk[l, rows].astype(jnp.float32)
            vv = xv[l, rows].astype(jnp.float32)
            stage[pl.ds(i * 512, 512), :] = jnp.concatenate([kk, vv], axis=-1).reshape(512, 128)
        for h in range(N):
            send[l, c, h] = stage[pl.ds(h, 128, stride=8), :].astype(jnp.bfloat16).reshape(8, 16, 128)

    def a2a_copy(l, c, d):
        t = peers[d]
        return pltpu.make_async_remote_copy(
            src_ref=send.at[l, c, t], dst_ref=recv.at[l, c, me],
            send_sem=a2a_ss.at[l, c, d], recv_sem=a2a_rs.at[l, c, d],
            device_id=dev(t), device_id_type=pl.DeviceIdType.MESH)

    def a2a_send(l, c):
        for d in range(N - 1):
            a2a_copy(l, c, d).start()
        recv[l, c, me] = send[l, c, me]

    def a2a_wait(l, c):
        for d in range(N - 1):
            a2a_copy(l, c, d).wait_recv()

    prep(0, 0)
    pl.semaphore_wait(barrier, N - 1)
    a2a_send(0, 0)
    for c in range(1, CH):
        prep(0, c)
        a2a_send(0, c)

    for cp in small_cp:
        cp.wait()
    for l in range(2):
        wqkv[l, pl.ds(256, 64), :] = jnp.zeros((64, D), jnp.bfloat16)
    qs[...] = jnp.zeros_like(qs)

    def rope_rows(b, _):
        pos = len_s[b]
        cos_b[pl.ds(b, 1), :] = cos_t[pl.ds(pos, 1), :]
        sin_b[pl.ds(b, 1), :] = sin_t[pl.ds(pos, 1), :]
        return 0
    lax.fori_loop(0, B, rope_rows, 0)

    for l in range(2):
        ids = lax.broadcasted_iota(jnp.int32, (128, B), 0)
        picked = jnp.zeros((128, B), jnp.float32)
        for k in range(8):
            picked = jnp.where(ids == choice_v[l, pl.ds(k, 1), :], 1.0, picked)
        mask_s[l] = picked.T

    lane = lax.broadcasted_iota(jnp.int32, (B, 128), 1)
    left = lane < 64
    lower = (lane % 64) < 32

    def norm_into(src, gain_ref, l):
        for hf in range(2):
            xs = [hb[src, 4 * hf + c].astype(jnp.float32) for c in range(4)]
            sq = xs[0] * xs[0]
            for x in xs[1:]:
                sq = sq + x * x
            scale = lax.rsqrt(jnp.sum(sq, axis=-1, keepdims=True) * (1.0 / D) + EPS)
            for c in range(4):
                g = gain_ref[pl.ds(l, 1), pl.ds(384 * c, 384)].astype(jnp.float32)
                m_s[pl.ds(16 * hf, 16), pl.ds(384 * c, 384)] = (xs[c] * scale * g).astype(jnp.bfloat16)

    def rope(x):
        rot = jnp.where(lower, -pltpu.roll(x, 96, 1), pltpu.roll(x, 32, 1))
        return x * cos_b[...] + rot * sin_b[...]

    def rounded(x):
        return x.astype(jnp.bfloat16).astype(jnp.float32)

    def project(l, src):
        norm_into(src, ga, l)
        qkv = dot_nt(m_s[...], wqkv[l])
        qa = rounded(rope(qkv[:, 0:128]))
        kq = rounded(rope(qkv[:, 128:256]))
        zero = jnp.zeros_like(qa)
        qs[pl.ds(0, B, stride=8), :] = jnp.where(left, qa, zero)
        qs[pl.ds(1, B, stride=8), :] = jnp.where(left, pltpu.roll(qa, 64, 1), zero)
        qs[pl.ds(2, B, stride=8), :] = jnp.where(left, pltpu.roll(kq, 64, 1), zero)
        kvn[...] = jnp.where(left, kq, rounded(qkv[:, 256:384]))

    row_ids = lax.broadcasted_iota(jnp.int32, (SEQ, 128), 0)
    lane8 = lax.broadcasted_iota(jnp.int32, (8, 128), 1)

    def attend(l):
        def chunk(c, _):
            a2a_wait(l, c)
            tiles, scores = [], []
            for i in range(8):
                b = c * 8 + i
                pos = len_s[b]
                tile = recv[l, c, :, i].reshape(SEQ, 128).astype(jnp.float32)
                tile = jnp.where(row_ids == pos, kvn[pl.ds(b, 1), :], tile).astype(jnp.bfloat16)
                recv[l, c, :, i] = tile.reshape(8, 16, 128)
                q = qs[pl.ds(pl.multiple_of(b * 8, 8), 8), :].astype(jnp.bfloat16)
                scores.append(jnp.where(lane8 <= pos, dot_nt(q, tile) * 0.125, -1e30))
                tiles.append(tile)
            s = jnp.concatenate(scores, axis=0)
            e = jnp.exp(s - jnp.max(s, axis=-1, keepdims=True))
            p = e / jnp.sum(e, axis=-1, keepdims=True)
            for i in range(8):
                b = c * 8 + i
                o = dot_nn(p[8 * i:8 * i + 8].astype(jnp.bfloat16), tiles[i])
                os_[pl.ds(pl.multiple_of(b * 8, 8), 8), :] = o
            return 0
        lax.fori_loop(0, CH, chunk, 0)

    def attn_out(l, ar):
        o0 = os_[pl.ds(0, B, stride=8), :]
        o1 = os_[pl.ds(1, B, stride=8), :]
        o2 = os_[pl.ds(2, B, stride=8), :]
        oa = jnp.where(left, pltpu.roll(o0, 64, 1), o1).astype(jnp.bfloat16)
        ob = pltpu.roll(o2, 64, 1)[:, 0:64].astype(jnp.bfloat16)
        part = dot_nn(oa, wo[l, pl.ds(0, 128)]) + dot_nn(ob, wo[l, pl.ds(128, 64)])
        put_partial(ar, part)

    def put_partial(ar, part):
        for j in range(N):
            psend[ar, j] = part[16 * (j // 4):16 * (j // 4) + 16, 384 * (j % 4):384 * (j % 4) + 384].astype(jnp.bfloat16)

    def rs_copy(ar, d):
        t = peers[d]
        return pltpu.make_async_remote_copy(
            src_ref=psend.at[ar, t], dst_ref=rsb.at[ar, d],
            send_sem=rs_ss.at[ar, d], recv_sem=rs_rs.at[ar, d],
            device_id=dev(t), device_id_type=pl.DeviceIdType.MESH)

    def ag_copy(ar, d):
        t = peers[d]
        return pltpu.make_async_remote_copy(
            src_ref=hb.at[ar + 1, me], dst_ref=hb.at[ar + 1, me],
            send_sem=ag_ss.at[ar, d], recv_sem=ag_rs.at[ar, d],
            device_id=dev(t), device_id_type=pl.DeviceIdType.MESH)

    def reduce_all(ar, filler=None):
        for d in range(N - 1):
            rs_copy(ar, d).start()
        if filler is not None:
            filler()
        total = psend[ar, me].astype(jnp.float32)
        for d in reversed(range(N - 1)):
            rs_copy(ar, d).wait_recv()
            total = total + rsb[ar, d].astype(jnp.float32)
        hb[ar + 1, me] = (hb[ar, me].astype(jnp.float32) + total).astype(jnp.bfloat16)
        for d in range(N - 1):
            ag_copy(ar, d).start()

    def gather_wait(ar):
        for d in range(N - 1):
            ag_copy(ar, d).wait_recv()

    out_refs = (kv1_o, kv2_o)

    def out_copy(l, c):
        return pltpu.make_async_copy(outs.at[l, pl.ds(c * 8, 8)], out_refs[l].at[pl.ds(c * 8, 8)], s_out.at[l, c])

    def write_caches(l):
        def chunk(c, _):
            for i in range(8):
                outs[l, c * 8 + i] = recv[l, c, :, i].reshape(SEQ, 128).T
            out_copy(l, c).start()
            return 0
        lax.fori_loop(0, CH, chunk, 0)

    lane_w = lax.broadcasted_iota(jnp.int32, (B, 128), 1) < 64

    def experts(l, ar):
        norm_into(ar, gm, l)
        logits = dot_nt(m_s[...], wr[l])
        chosen = mask_s[l][:, 0:40] > 0.5
        top = jnp.max(jnp.where(chosen, logits, -jnp.inf), axis=-1, keepdims=True)
        e = jnp.where(chosen, jnp.exp(jnp.where(chosen, logits - top, 0.0)), 0.0)
        gate = e / jnp.sum(e, axis=-1, keepdims=True)
        for j in range(QUADS):
            for i in range(2):
                k = 4 * j + 2 * i
                g0 = jnp.broadcast_to(gate[:, k:k + 1], (B, 128))
                g1 = jnp.broadcast_to(gate[:, k + 1:k + 2], (B, 128))
                gx[j, :, pl.ds(128 * i, 128)] = jnp.where(lane_w, g0, g1)

        def up(j):
            rows = pl.ds(pl.multiple_of(j * 256, 256), 256)
            cps = weight_copies(l, j)
            for cp in cps:
                cp.wait()
            g = dot_nt(m_s[...], wg[l, rows, :])
            u = dot_nt(m_s[...], wu[l, rows, :])
            act[j] = (gx[j] * (g * jax.nn.sigmoid(g)) * u).astype(jnp.bfloat16)

        def down(j):
            rows = pl.ds(pl.multiple_of(j * 256, 256), 256)
            return dot_nn(act[j], wd[l, rows, :])

        acc[...] = jnp.zeros_like(acc)
        up(0)

        def step(j, _):
            up(j)
            acc[...] += down(j - 1)
            return 0
        lax.fori_loop(1, QUADS, step, 0)
        put_partial(ar, acc[...] + down(QUADS - 1))

    prep(1, 0)
    a2a_send(1, 0)
    project(0, 0)
    for c in range(1, CH):
        prep(1, c)
    attend(0)
    attn_out(0, 0)
    reduce_all(0, lambda: write_caches(0))
    gather_wait(0)
    for c in range(1, CH):
        a2a_send(1, c)
    experts(0, 1)
    reduce_all(1)
    gather_wait(1)
    project(1, 2)
    attend(1)
    attn_out(1, 2)
    reduce_all(2, lambda: write_caches(1))
    gather_wait(2)
    experts(1, 3)
    reduce_all(3)
    gather_wait(3)

    hid_cp = [pltpu.make_async_copy(hb.at[4, j], hid_o.at[pl.ds(16 * (j // 4), 16), pl.ds(384 * (j % 4), 384)], s_small.at[j]) for j in range(N)]
    for cp in hid_cp:
        cp.start()
    for l in range(2):
        for c in range(CH):
            out_copy(l, c).wait()
            for d in range(N - 1):
                a2a_copy(l, c, d).wait_send()
    for ar in range(4):
        for d in range(N - 1):
            rs_copy(ar, d).wait_send()
            ag_copy(ar, d).wait_send()
    for cp in hid_cp:
        cp.wait()


def solution(mesh):
    seq_spec = P('dp', 'tp', None, None)
    head_spec = P('dp', None, 'tp', None)
    col_spec = P(None, None, 'tp')
    ff_spec = P(None, None, None, 'tp')
    cos, sin = rope_tables()

    def local_step(hidden, lengths, choice, keys_one, vals_one, keys_two, vals_two, g_attn, w_q, w_k, w_v, w_o, g_mlp, w_router, w_gate, w_up, w_down):
        bf, f32 = jnp.bfloat16, jnp.float32
        any_spec = pl.BlockSpec(memory_space=pl.ANY)
        dma = pltpu.SemaphoreType.DMA
        vm = pltpu.VMEM
        operands = (
            lengths, hidden, jnp.swapaxes(choice, 1, 2),
            keys_one.reshape(512, 8, 64), vals_one.reshape(512, 8, 64), keys_two.reshape(512, 8, 64), vals_two.reshape(512, 8, 64),
            g_attn, jnp.swapaxes(w_q, 1, 2), jnp.swapaxes(w_k, 1, 2), jnp.swapaxes(w_v, 1, 2), w_o, g_mlp, jnp.swapaxes(w_router, 1, 2),
            jnp.swapaxes(w_gate, 2, 3).reshape(2, 2560, D), jnp.swapaxes(w_up, 2, 3).reshape(2, 2560, D), w_down.reshape(2, 2560, D),
            jnp.asarray(cos), jnp.asarray(sin),
        )
        hid, kv1, kv2 = pl.pallas_call(
            kernel,
            name='decode_two',
            out_shape=[jax.ShapeDtypeStruct((B, D), bf), jax.ShapeDtypeStruct((B, 128, 128), bf), jax.ShapeDtypeStruct((B, 128, 128), bf)],
            in_specs=[pl.BlockSpec(memory_space=pltpu.SMEM)] + [any_spec] * 18,
            out_specs=[any_spec] * 3,
            scratch_shapes=[
                vm((2, 2560, D), bf), vm((2, 2560, D), bf), vm((2, 2560, D), bf),
                vm((2, 384, D), bf), vm((2, 192, D), bf), vm((2, 40, D), bf),
                vm((2, 512, 8, 64), bf), vm((2, 512, 8, 64), bf), vm((1024, 128), f32),
                vm((2, CH, 8, 8, 16, 128), bf), vm((2, CH, 8, 8, 16, 128), bf), vm((2, B, 128, 128), bf),
                vm((5, 8, 16, 384), bf), vm((4, 8, 16, 384), bf), vm((4, 7, 16, 384), bf),
                vm((B, D), bf), vm((256, 128), f32), vm((8, 128), f32), vm((256, 128), f32), vm((B, 128), f32),
                vm((128, 128), f32), vm((128, 128), f32), vm((B, 128), f32), vm((B, 128), f32),
                vm((2, 8, B), jnp.int32), vm((2, D), bf), vm((2, D), bf),
                vm((2, B, 128), f32), vm((QUADS, B, 256), f32), vm((QUADS, B, 256), bf), vm((B, D), f32),
                dma((2, CH, 2)), dma((2, QUADS, 3)), dma((23,)), dma((2, CH)),
                dma((2, CH, 7)), dma((2, CH, 7)), dma((4, 7)), dma((4, 7)), dma((4, 7)), dma((4, 7)),
            ],
            compiler_params=pltpu.CompilerParams(collective_id=0, has_side_effects=True, vmem_limit_bytes=67043328),
        )(*operands)
        outs = []
        for kv in (kv1, kv2):
            outs.append(jnp.swapaxes(kv[:, 0:64], 1, 2)[:, :, None, :])
            outs.append(jnp.swapaxes(kv[:, 64:128], 1, 2)[:, :, None, :])
        return (hid, outs[0], outs[1], outs[2], outs[3])

    return jax.shard_map(local_step, mesh=mesh, in_specs=(P('dp', None), P('dp'), P(None, 'dp', None), seq_spec, seq_spec, seq_spec, seq_spec, P(), col_spec, col_spec, col_spec, P(None, 'tp', None), P(), P(), ff_spec, ff_spec, P(None, None, 'tp', None)), out_specs=(P('dp', None), head_spec, head_spec, head_spec, head_spec), check_vma=False)
```

time: 288 us -> 75.1 us (0.26)
  waiting for transfers between devices: 165 us -> 0 us
  Pallas kernels: 0 us -> 69.9 us
  matrix products: 49.6 us -> 0 us
  local copies, waits for them, and re-layouts: 30.4 us -> 4.42 us
  other arithmetic: 14.5 us -> 0 us
  starting transfers between devices: 13.6 us -> 0 us
  between operations: 14.2 us -> 0.65 us
    psum x4 -> x0, waiting for transfers between devices: 145 us -> none  [the longest x2 77.4 us: decode_layer(): lax.psum(jnp.dot(attn_vec, w_o, preferred_element_type=jnp.float32).astyp...]
    pallas_call x0 -> x1, Pallas kernels: none -> 69.9 us  [local_step(): pl.pallas_call(kernel, name='decode_two', out_shape=[jax.ShapeDtypeStruct...]
    dot_general x18 -> x0, matrix products: 49.6 us -> none  [the longest x2 18.6 us: expert_block(): jnp.einsum('bef,efd->bd', expert_in, w_down, preferred_element_type=jnp.f...]
    unnamed x40 -> x2, local copies, waits for them, and re-layouts: 26.9 us -> 4.42 us
    all_to_all x4 -> x0, waiting for transfers between devices: 19.3 us -> none  [local_step(): lax.all_to_all(cache_blk, 'tp', 2, 1, tiled=True)]
    all_to_all x4 -> x0, starting transfers between devices: 13 us -> none  [local_step(): lax.all_to_all(cache_blk, 'tp', 2, 1, tiled=True)]
    select_n x1 -> x0, other arithmetic: 5.13 us -> none  [decode_layer(): val_cache = jnp.where(is_new, val_new[:, None], val_cache)]
    reduce_sum x10 -> x0, other arithmetic: 4 us -> none  [the longest x4 3.24 us: rms_norm(): jnp.mean(tensor_f * tensor_f, axis=-1, keepdims=True) + EPS]
  transfers between devices with their start and end apart: 8 -> 0, of which waited for: 7 -> 0; matrix products, arithmetic and copies ran while one was open for 14% -> 0% of each run, Pallas kernels for 0% -> 0%
where the time goes in v1:
time: 75.1 us; the launch traced here: 74.9 us
  Pallas kernels  69.9 us (93%)
  local copies, waits for them, and re-layouts  4.42 us (6%)
    pallas_call x1, Pallas kernels, local_step(): pl.pallas_call(kernel, name='decode_two', out_shape=[jax.ShapeDtypeStruct...  69.9 us
    unnamed x2, local copies, waits for them, and re-layouts  4.42 us

profile of v1, /device:TPU:0, one launch (start us, length us, event | category | flops | bytes accessed | tf_op | source)
XLA Modules:
  0.0 74.9 jit_solution(13167585769184131333)
XLA Ops:
  0.6 69.9 %decode_two.1 = (bf16[32,1536]{1,0:T(8,128)(2,1)}, bf16[32,128,128]{2,1,0:T(8,128)(2,1)}, bf16[32,128,128]{2,1,0:T(8,128)(2,1)}) custom-call(s32[32]{0:T(128)} %len_s.1, bf16[32,1536]{1,0:T(8,128)(2,1)} %hid_h.1, s32[2,8,32]{2,1,0:T(8,128)} %bitcast.51, bf16[512,8,64]{2,1,0:T(8,128)(2,1)} %bitcast.44, bf16[512,8,64]{2,1,0:T(8,128)(2,1)} %bitcast.45, ...), custom_call_target="tpu_custom_call" | custom-call | tf_op jit(solution)/shard_map/decode_two/pallas_call | solution.py:364
  70.5 2.9 %slice_bitcast_fusion = (bf16[32,128,1,64]{1,3,2,0:T(8,128)(2,1)}, bf16[32,128,1,64]{1,3,2,0:T(8,128)(2,1)}, bf16[32,128,1,64]{1,3,2,0:T(8,128)(2,1)}, bf16[32,128,1,64]{1,3,2,0:T(8,128)(2,1)}) fusion(bf16[32,128,128]{2,1,0:T(8,128)(2,1)} %get-tuple-element.10, bf16[32,128,128]{2,1,0:T(8,128)(2,1)} %get-tuple-element.9), kind=kLoop, calls=%fused_computation | loop fusion | bytes 4194304
  73.4 1.5 %copy.29 = bf16[32,1536]{1,0:T(8,128)(2,1)} copy(bf16[32,1536]{1,0:T(8,128)(2,1)} %get-tuple-element.27) | data formatting | bytes 196608

commit v2 on v1

--- a/solution.py
+++ b/solution.py
@@ -36,9 +36,9 @@
 
 
 def kernel(len_s, hid_h, choice_h, k1_h, v1_h, k2_h, v2_h, ga_h, wq_h, wk_h, wv_h, wo_h, gm_h, wr_h, wg_h, wu_h, wd_h, cos_h, sin_h,
-           hid_o, kv1_o, kv2_o,
-           wg, wu, wd, wqkv, wo, wr, xk, xv, stage, send, recv, outs, hb, psend, rsb, m_s, qs, sc, os_, kvn, cos_t, sin_t, cos_b, sin_b, choice_v, ga, gm, mask_s, gx, act, acc,
-           s_in, s_w, s_small, s_out, a2a_ss, a2a_rs, rs_ss, rs_rs, ag_ss, ag_rs):
+           hid_o, outs1, outs2,
+           wg, wu, wd, wqkv, wo, wr, xk, xv, stage, send, recv, hb, psend, rsb, m_s, qs, sc, os_, kvn, cos_t, sin_t, cos_b, sin_b, choice_v, ga, gm, mask_s, gx, act, acc,
+           s_in, s_w, s_small, a2a_ss, a2a_rs, ar_ss, rs_rs, ag_rs):
     me = lax.axis_index('tp')
     my, mx, mc = me // 4, (me // 2) % 2, me % 2
     peers = []
@@ -47,6 +47,9 @@
 
     def dev(t):
         return {'tp': t}
+
+    def landed(like, sem):
+        pltpu.make_async_copy(like, like, sem).wait()
 
     barrier = pltpu.get_barrier_semaphore()
     for t in peers:
@@ -58,7 +61,7 @@
         for c in range(CH):
             for i, buf in enumerate((xk, xv)):
                 rows = pl.ds(c * 128, 128)
-                cp = pltpu.make_async_copy(caches[l][i].at[rows], buf.at[l, rows], s_in.at[l, c, i])
+                cp = pltpu.make_async_copy(caches[l][i].at[rows], buf.at[l, rows], s_in.at[l, c])
                 cache_cp[l, c, i] = cp
 
     small = [
@@ -71,7 +74,7 @@
         small.append((wv_h.at[l], wqkv.at[l, pl.ds(320, 64)]))
     for j in range(N):
         small.append((hid_h.at[pl.ds(16 * (j // 4), 16), pl.ds(384 * (j % 4), 384)], hb.at[0, j]))
-    small_cp = [pltpu.make_async_copy(src, dst, s_small.at[i]) for i, (src, dst) in enumerate(small)]
+    small_cp = [pltpu.make_async_copy(src, dst, s_small) for src, dst in small]
 
     for c in range(CH):
         cache_cp[0, c, 0].start()
@@ -84,8 +87,8 @@
 
     def weight_copies(l, j):
         rows = pl.ds(pl.multiple_of(j * 256, 256), 256)
-        return [pltpu.make_async_copy(src.at[l, rows], dst.at[l, rows], s_w.at[l, j, i])
-                for i, (src, dst) in enumerate(((wg_h, wg), (wu_h, wu), (wd_h, wd)))]
+        return [pltpu.make_async_copy(src.at[l, rows], dst.at[l, rows], s_w.at[l, j])
+                for src, dst in ((wg_h, wg), (wu_h, wu), (wd_h, wd))]
 
     for l in range(2):
         def start_weights(j, _, l=l):
@@ -95,8 +98,7 @@
         lax.fori_loop(0, QUADS, start_weights, 0)
 
     def prep(l, c):
-        cache_cp[l, c, 0].wait()
-        cache_cp[l, c, 1].wait()
+        landed(xk.at[l, pl.ds(0, 256)], s_in.at[l, c])
         for i in range(2):
             rows = pl.ds(c * 128 + i * 64, 64)
             kk = xk[l, rows].astype(jnp.float32)
@@ -109,7 +111,7 @@
         t = peers[d]
         return pltpu.make_async_remote_copy(
             src_ref=send.at[l, c, t], dst_ref=recv.at[l, c, me],
-            send_sem=a2a_ss.at[l, c, d], recv_sem=a2a_rs.at[l, c, d],
+            send_sem=a2a_ss, recv_sem=a2a_rs.at[l, c],
             device_id=dev(t), device_id_type=pl.DeviceIdType.MESH)
 
     def a2a_send(l, c):
@@ -118,8 +120,7 @@
         recv[l, c, me] = send[l, c, me]
 
     def a2a_wait(l, c):
-        for d in range(N - 1):
-            a2a_copy(l, c, d).wait_recv()
+        landed(recv.at[l, c, pl.ds(0, N - 1)], a2a_rs.at[l, c])
 
     prep(0, 0)
     pl.semaphore_wait(barrier, N - 1)
@@ -224,14 +225,14 @@
         t = peers[d]
         return pltpu.make_async_remote_copy(
             src_ref=psend.at[ar, t], dst_ref=rsb.at[ar, d],
-            send_sem=rs_ss.at[ar, d], recv_sem=rs_rs.at[ar, d],
+            send_sem=ar_ss, recv_sem=rs_rs.at[ar],
             device_id=dev(t), device_id_type=pl.DeviceIdType.MESH)
 
     def ag_copy(ar, d):
         t = peers[d]
         return pltpu.make_async_remote_copy(
             src_ref=hb.at[ar + 1, me], dst_ref=hb.at[ar + 1, me],
-            send_sem=ag_ss.at[ar, d], recv_sem=ag_rs.at[ar, d],
+            send_sem=ar_ss, recv_sem=ag_rs.at[ar],
             device_id=dev(t), device_id_type=pl.DeviceIdType.MESH)
 
     def reduce_all(ar, filler=None):
@@ -240,27 +241,22 @@
         if filler is not None:
             filler()
         total = psend[ar, me].astype(jnp.float32)
-        for d in reversed(range(N - 1)):
-            rs_copy(ar, d).wait_recv()
+        landed(rsb.at[ar], rs_rs.at[ar])
+        for d in range(N - 1):
             total = total + rsb[ar, d].astype(jnp.float32)
         hb[ar + 1, me] = (hb[ar, me].astype(jnp.float32) + total).astype(jnp.bfloat16)
         for d in range(N - 1):
             ag_copy(ar, d).start()
 
     def gather_wait(ar):
-        for d in range(N - 1):
-            ag_copy(ar, d).wait_recv()
-
-    out_refs = (kv1_o, kv2_o)
-
-    def out_copy(l, c):
-        return pltpu.make_async_copy(outs.at[l, pl.ds(c * 8, 8)], out_refs[l].at[pl.ds(c * 8, 8)], s_out.at[l, c])
+        landed(rsb.at[ar], ag_rs.at[ar])
+
+    out_refs = (outs1, outs2)
 
     def write_caches(l):
         def chunk(c, _):
             for i in range(8):
-                outs[l, c * 8 + i] = recv[l, c, :, i].reshape(SEQ, 128).T
-            out_copy(l, c).start()
+                out_refs[l][c * 8 + i] = recv[l, c, :, i].reshape(SEQ, 128).T
             return 0
         lax.fori_loop(0, CH, chunk, 0)
 
@@ -282,9 +278,7 @@
 
         def up(j):
             rows = pl.ds(pl.multiple_of(j * 256, 256), 256)
-            cps = weight_copies(l, j)
-            for cp in cps:
-                cp.wait()
+            landed(wg.at[l, pl.ds(0, 768)], s_w.at[l, j])
             g = dot_nt(m_s[...], wg[l, rows, :])
             u = dot_nt(m_s[...], wu[l, rows, :])
             act[j] = (gx[j] * (g * jax.nn.sigmoid(g)) * u).astype(jnp.bfloat16)
@@ -303,42 +297,66 @@
         lax.fori_loop(1, QUADS, step, 0)
         put_partial(ar, acc[...] + down(QUADS - 1))
 
-    prep(1, 0)
-    a2a_send(1, 0)
-    project(0, 0)
-    for c in range(1, CH):
-        prep(1, c)
-    attend(0)
-    attn_out(0, 0)
-    reduce_all(0, lambda: write_caches(0))
-    gather_wait(0)
+    SC = jax.named_scope
+    with SC("p_prep1"):
+        prep(1, 0)
+        a2a_send(1, 0)
+    with SC("p_proj0"):
+        project(0, 0)
+    with SC("p_prep1b"):
+        for c in range(1, CH):
+            prep(1, c)
+    with SC("p_att0"):
+        attend(0)
+    with SC("p_aout0"):
+        attn_out(0, 0)
+    with SC("p_rs0"):
+        reduce_all(0, lambda: write_caches(0))
+    with SC("p_ag0"):
+        gather_wait(0)
     for c in range(1, CH):
         a2a_send(1, c)
-    experts(0, 1)
-    reduce_all(1)
-    gather_wait(1)
-    project(1, 2)
-    attend(1)
-    attn_out(1, 2)
-    reduce_all(2, lambda: write_caches(1))
-    gather_wait(2)
-    experts(1, 3)
-    reduce_all(3)
-    gather_wait(3)
-
-    hid_cp = [pltpu.make_async_copy(hb.at[4, j], hid_o.at[pl.ds(16 * (j // 4), 16), pl.ds(384 * (j % 4), 384)], s_small.at[j]) for j in range(N)]
-    for cp in hid_cp:
+    with SC("p_moe0"):
+        experts(0, 1)
+    with SC("p_rs1"):
+        reduce_all(1)
+    with SC("p_ag1"):
+        gather_wait(1)
+    with SC("p_proj1"):
+        project(1, 2)
+    with SC("p_att1"):
+        attend(1)
+    with SC("p_aout1"):
+        attn_out(1, 2)
+    with SC("p_rs2"):
+        reduce_all(2, lambda: write_caches(1))
+    with SC("p_ag2"):
+        gather_wait(2)
+    with SC("p_moe1"):
+        experts(1, 3)
+    with SC("p_rs3"):
+        reduce_all(3)
+    with SC("p_ag3"):
+        gather_wait(3)
+
+    with SC("p_end"):
+        for j in range(N):
+            hid_o[pl.ds(16 * (j // 4), 16), pl.ds(384 * (j % 4), 384)] = hb[4, j]
+        landed(send.at[:, :, pl.ds(0, N - 1)], a2a_ss)
+        landed(rsb, ar_ss)
+        landed(rsb, ar_ss)
+
+
+def tail_kernel(hid, kv1, kv2, hid_o, k1_o, v1_o, k2_o, v2_o, sem):
+    copies = [
+        (kv1.at[:, pl.ds(0, 64)], k1_o), (kv1.at[:, pl.ds(64, 64)], v1_o),
+        (kv2.at[:, pl.ds(0, 64)], k2_o), (kv2.at[:, pl.ds(64, 64)], v2_o),
+        (hid, hid_o),
+    ]
+    cps = [pltpu.make_async_copy(src, dst, sem.at[i]) for i, (src, dst) in enumerate(copies)]
+    for cp in cps:
         cp.start()
-    for l in range(2):
-        for c in range(CH):
-            out_copy(l, c).wait()
-            for d in range(N - 1):
-                a2a_copy(l, c, d).wait_send()
-    for ar in range(4):
-        for d in range(N - 1):
-            rs_copy(ar, d).wait_send()
-            ag_copy(ar, d).wait_send()
-    for cp in hid_cp:
+    for cp in cps:
         cp.wait()
 
 
@@ -352,6 +370,7 @@
     def local_step(hidden, lengths, choice, keys_one, vals_one, keys_two, vals_two, g_attn, w_q, w_k, w_v, w_o, g_mlp, w_router, w_gate, w_up, w_down):
         bf, f32 = jnp.bfloat16, jnp.float32
         any_spec = pl.BlockSpec(memory_space=pl.ANY)
+        vmem_spec = pl.BlockSpec(memory_space=pltpu.VMEM)
         dma = pltpu.SemaphoreType.DMA
         vm = pltpu.VMEM
         operands = (
@@ -364,28 +383,32 @@
         hid, kv1, kv2 = pl.pallas_call(
             kernel,
             name='decode_two',
-            out_shape=[jax.ShapeDtypeStruct((B, D), bf), jax.ShapeDtypeStruct((B, 128, 128), bf), jax.ShapeDtypeStruct((B, 128, 128), bf)],
+            out_shape=[vm((B, D), bf), vm((B, 128, 128), bf), vm((B, 128, 128), bf)],
             in_specs=[pl.BlockSpec(memory_space=pltpu.SMEM)] + [any_spec] * 18,
-            out_specs=[any_spec] * 3,
+            out_specs=[vmem_spec] * 3,
             scratch_shapes=[
                 vm((2, 2560, D), bf), vm((2, 2560, D), bf), vm((2, 2560, D), bf),
                 vm((2, 384, D), bf), vm((2, 192, D), bf), vm((2, 40, D), bf),
                 vm((2, 512, 8, 64), bf), vm((2, 512, 8, 64), bf), vm((1024, 128), f32),
-                vm((2, CH, 8, 8, 16, 128), bf), vm((2, CH, 8, 8, 16, 128), bf), vm((2, B, 128, 128), bf),
+                vm((2, CH, 8, 8, 16, 128), bf), vm((2, CH, 8, 8, 16, 128), bf),
                 vm((5, 8, 16, 384), bf), vm((4, 8, 16, 384), bf), vm((4, 7, 16, 384), bf),
                 vm((B, D), bf), vm((256, 128), f32), vm((8, 128), f32), vm((256, 128), f32), vm((B, 128), f32),
                 vm((128, 128), f32), vm((128, 128), f32), vm((B, 128), f32), vm((B, 128), f32),
                 vm((2, 8, B), jnp.int32), vm((2, D), bf), vm((2, D), bf),
                 vm((2, B, 128), f32), vm((QUADS, B, 256), f32), vm((QUADS, B, 256), bf), vm((B, D), f32),
-                dma((2, CH, 2)), dma((2, QUADS, 3)), dma((23,)), dma((2, CH)),
-                dma((2, CH, 7)), dma((2, CH, 7)), dma((4, 7)), dma((4, 7)), dma((4, 7)), dma((4, 7)),
+                dma((2, CH)), dma((2, QUADS)), dma, dma, dma((2, CH)), dma, dma((4,)), dma((4,)),
             ],
-            compiler_params=pltpu.CompilerParams(collective_id=0, has_side_effects=True, vmem_limit_bytes=67043328),
+            compiler_params=pltpu.CompilerParams(collective_id=0, has_side_effects=True, vmem_limit_bytes=63500000),
         )(*operands)
-        outs = []
-        for kv in (kv1, kv2):
-            outs.append(jnp.swapaxes(kv[:, 0:64], 1, 2)[:, :, None, :])
-            outs.append(jnp.swapaxes(kv[:, 64:128], 1, 2)[:, :, None, :])
-        return (hid, outs[0], outs[1], outs[2], outs[3])
+        hid_out, *caches = pl.pallas_call(
+            tail_kernel,
+            name='write_out',
+            out_shape=[jax.ShapeDtypeStruct((B, D), bf)] + [jax.ShapeDtypeStruct((B, 64, 128), bf)] * 4,
+            in_specs=[vmem_spec] * 3,
+            out_specs=[any_spec] * 5,
+            scratch_shapes=[dma((5,))],
+            compiler_params=pltpu.CompilerParams(vmem_limit_bytes=4 << 20),
+        )(hid, kv1, kv2)
+        return (hid_out, *[jnp.swapaxes(kv, 1, 2)[:, :, None, :] for kv in caches])
 
     return jax.shard_map(local_step, mesh=mesh, in_specs=(P('dp', None), P('dp'), P(None, 'dp', None), seq_spec, seq_spec, seq_spec, seq_spec, P(), col_spec, col_spec, col_spec, P(None, 'tp', None), P(), P(), ff_spec, ff_spec, P(None, None, 'tp', None)), out_specs=(P('dp', None), head_spec, head_spec, head_spec, head_spec), check_vma=False)

time: 75.1 us -> 68.7 us (0.915)
  local copies, waits for them, and re-layouts: 4.42 us -> 0 us
  Pallas kernels: 69.9 us -> 68 us
    unnamed x2 -> x0, local copies, waits for them, and re-layouts: 4.42 us -> none
    pallas_call x1 -> x2, Pallas kernels: 69.9 us -> 68 us  [the longest x1 66.6 us: local_step(): pl.pallas_call(kernel, name='decode_two', out_shape=[vm((B, D), bf), vm((...]
where the time goes in v2:
time: 68.7 us; the launch traced here: 68.6 us
  Pallas kernels  68 us (99%)
    pallas_call x1, Pallas kernels, local_step(): pl.pallas_call(kernel, name='decode_two', out_shape=[vm((B, D), bf), vm((...  66.6 us
    pallas_call x1, Pallas kernels, local_step(): pl.pallas_call(tail_kernel, name='write_out', out_shape=[jax.ShapeDtypeSt...  1.38 us

profile of v2, /device:TPU:0, one launch (start us, length us, event | category | flops | bytes accessed | tf_op | source)
XLA Modules:
  0.0 68.6 jit_solution(13626077338925421199)
XLA Ops:
  0.6 66.6 %decode_two.1 = (bf16[32,1536]{1,0:T(8,128)(2,1)S(1)}, bf16[32,128,128]{2,1,0:T(8,128)(2,1)S(1)}, bf16[32,128,128]{2,1,0:T(8,128)(2,1)S(1)}) custom-call(s32[32]{0:T(128)} %len_s.1, bf16[32,1536]{1,0:T(8,128)(2,1)} %hid_h.1, s32[2,8,32]{2,1,0:T(8,128)} %bitcast.47, bf16[512,8,64]{2,1,0:T(8,128)(2,1)} %bitcast.40, bf16[512,8,64]{2,1,0:T(8,128)(2,1)} %bitcast.41, ...), custom_call_target="tpu_custom_call" | custom-call | tf_op jit(solution)/shard_map/decode_two/pallas_call | solution.py:383
  67.3 1.4 %write_out.1 = (bf16[32,1536]{1,0:T(8,128)(2,1)}, bf16[32,64,128]{2,1,0:T(8,128)(2,1)}, bf16[32,64,128]{2,1,0:T(8,128)(2,1)}, bf16[32,64,128]{2,1,0:T(8,128)(2,1)}, bf16[32,64,128]{2,1,0:T(8,128)(2,1)}) custom-call(bf16[32,1536]{1,0:T(8,128)(2,1)S(1)} %get-tuple-element.13.hid, bf16[32,128,128]{2,1,0:T(8,128)(2,1)S(1)} %get-tuple-element.14.kv1, ...), custom_call_target="tpu_custom_call" | custom-call | tf_op jit(solution)/shard_map/write_out/pallas_call | solution.py:403

commit v3 on v2

v3 whole, which is shorter than its diff:
```python
import jax
import jax.numpy as jnp
import numpy as np
from jax import lax
from jax.experimental import pallas as pl
from jax.experimental.pallas import tpu as pltpu
from jax.sharding import PartitionSpec as P

EPS = 1e-5
THETA = 1000000.0
N = 8
B = 32
D = 1536
SEQ = 128
LANES, HEAD, ROWS, COLS, TILE, SLOTS, WIDE = 128, 64, 16, 384, 256, 512, 768
CH = 4
TP = 8
QUADS = 10
NT = (((1,), (1,)), ((), ()))
PEERS = ((1, 1, 0), (1, 1, 1), (1, 0, 1), (0, 1, 0), (1, 0, 0), (0, 1, 1), (0, 0, 1))


def rope_tables():
    half = 32
    inv = np.power(np.float32(THETA), (-2.0 * np.arange(half, dtype=np.float32) / HEAD).astype(np.float32)).astype(np.float32)
    angle = (np.arange(SEQ, dtype=np.float32)[:, None] * inv[None, :]).astype(np.float32).astype(np.float64)
    cos = np.tile(np.cos(angle), (1, 4)).astype(np.float32)
    sin = np.tile(np.sin(angle), (1, 4)).astype(np.float32)
    return cos, sin


def dot_nt(a, b):
    return lax.dot_general(a, b, NT, preferred_element_type=jnp.float32)


def dot_nn(a, b):
    return jnp.dot(a, b, preferred_element_type=jnp.float32)


def kernel(len_s, hid_h, choice_h, k1_h, v1_h, k2_h, v2_h, ga_h, wq_h, wk_h, wv_h, wo_h, gm_h, wr_h, wg_h, wu_h, wd_h, cos_h, sin_h,
           hid_o, outs1, outs2,
           wg, wu, wd, wqkv, wo, wr, xk, xv, stage, send, recv, hb, psend, rsb, m_s, qs, sc, os_, kvn, cos_t, sin_t, cos_b, sin_b, choice_v, ga, gm, mask_s, gx, act, acts,
           s_in, s_w, s_d, s_small, a2a_ss, a2a_rs, ar_ss, rs_rs, ag_rs):
    me = lax.axis_index('tp')
    my, mx, mc = me // 4, (me // 2) % 2, me % 2
    peers = []
    for dy, dx, dc in PEERS:
        peers.append(((my + dy) % 2) * 4 + ((mx + dx) % 2) * 2 + (mc + dc) % 2)

    def dev(t):
        return {'tp': t}

    def landed(like, sem):
        pltpu.make_async_copy(like, like, sem).wait()

    caches = ((k1_h, v1_h), (k2_h, v2_h))
    cache_cp = {}
    for l in range(2):
        for c in range(CH):
            for i, buf in enumerate((xk, xv)):
                rows = pl.ds(c * LANES, LANES)
                cp = pltpu.make_async_copy(caches[l][i].at[rows], buf.at[l, rows], s_in.at[l, c])
                cache_cp[l, c, i] = cp

    for c in range(CH):
        cache_cp[0, c, 0].start()
        cache_cp[0, c, 1].start()

    barrier = pltpu.get_barrier_semaphore()
    for t in peers:
        pl.semaphore_signal(barrier, inc=1, device_id=dev(t), device_id_type=pl.DeviceIdType.MESH)

    small = [
        (cos_h, cos_t), (sin_h, sin_t), (choice_h, choice_v), (ga_h, ga), (gm_h, gm), (wr_h, wr), (wo_h, wo),
    ]
    for l in range(2):
        small.append((wq_h.at[l, pl.ds(0, LANES)], wqkv.at[l, pl.ds(0, LANES)]))
        small.append((wk_h.at[l], wqkv.at[l, pl.ds(LANES, HEAD)]))
        small.append((wq_h.at[l, pl.ds(LANES, HEAD)], wqkv.at[l, pl.ds(192, HEAD)]))
        small.append((wv_h.at[l], wqkv.at[l, pl.ds(320, HEAD)]))
    for j in range(N):
        small.append((hid_h.at[pl.ds(ROWS * (j // 4), ROWS), pl.ds(COLS * (j % 4), COLS)], hb.at[0, j]))
    small_cp = [pltpu.make_async_copy(src, dst, s_small) for src, dst in small]

    def weight_rows(j):
        return pl.ds(pl.multiple_of(j * TILE, TILE), TILE)

    def start_rest():
        for cp in small_cp:
            cp.start()
        for c in range(CH):
            cache_cp[1, c, 0].start()
            cache_cp[1, c, 1].start()
        for l in range(2):
            def start_gate_up(j, _, l=l):
                rows = weight_rows(j)
                pltpu.make_async_copy(wg_h.at[l, rows], wg.at[l, rows], s_w.at[l, j]).start()
                pltpu.make_async_copy(wu_h.at[l, rows], wu.at[l, rows], s_w.at[l, j]).start()
                return 0
            lax.fori_loop(0, QUADS, start_gate_up, 0)
            def start_down(j, _, l=l):
                rows = weight_rows(j)
                pltpu.make_async_copy(wd_h.at[l, rows], wd.at[l, rows], s_d.at[l]).start()
                return 0
            lax.fori_loop(0, QUADS, start_down, 0)

    def prep(l, c):
        landed(xk.at[l, pl.ds(0, TILE)], s_in.at[l, c])
        for i in range(2):
            rows = pl.ds(c * LANES + i * HEAD, HEAD)
            kk = xk[l, rows].astype(jnp.float32)
            vv = xv[l, rows].astype(jnp.float32)
            stage[pl.ds(i * SLOTS, SLOTS), :] = jnp.concatenate([kk, vv], axis=-1).reshape(SLOTS, LANES)
        for h in range(N):
            rows = stage[pl.ds(h, LANES, stride=8), :].astype(jnp.bfloat16).reshape(2, 4, ROWS, LANES)
            send[l, 2 * c, h] = rows[0]
            send[l, 2 * c + 1, h] = rows[1]

    def a2a_copy(l, p, d):
        t = peers[d]
        return pltpu.make_async_remote_copy(
            src_ref=send.at[l, p, t], dst_ref=recv.at[l, p, me],
            send_sem=a2a_ss, recv_sem=a2a_rs.at[l, p],
            device_id=dev(t), device_id_type=pl.DeviceIdType.MESH)

    def a2a_send2(l, p):
        for d in range(N - 1):
            t = peers[d]
            pltpu.make_async_remote_copy(
                src_ref=send.at[l, pl.ds(p, 2), t], dst_ref=recv.at[l, pl.ds(p, 2), me],
                send_sem=a2a_ss, recv_sem=a2a_rs.at[l, p],
                device_id=dev(t), device_id_type=pl.DeviceIdType.MESH).start()
        recv[l, pl.ds(p, 2), me] = send[l, pl.ds(p, 2), me]

    def a2a_send(l, p):
        for d in range(N - 1):
            a2a_copy(l, p, d).start()
        recv[l, p, me] = send[l, p, me]

    def a2a_wait(l, p):
        landed(recv.at[l, p, pl.ds(0, N - 1)], a2a_rs.at[l, p])

    with jax.named_scope('p_prep0'):
        prep(0, 0)
    with jax.named_scope('p_bar'):
        pl.semaphore_wait(barrier, N - 1)
    with jax.named_scope('p_send0'):
        a2a_send2(0, 0)
        for c in range(1, CH):
            prep(0, c)
            a2a_send2(0, 2 * c)
    with jax.named_scope('p_rest'):
        start_rest()

    for cp in small_cp:
        cp.wait()
    for l in range(2):
        wqkv[l, pl.ds(TILE, HEAD), :] = jnp.zeros((HEAD, D), jnp.bfloat16)
    qs[...] = jnp.zeros_like(qs)

    def rope_rows(b, _):
        pos = len_s[b]
        cos_b[pl.ds(b, 1), :] = cos_t[pl.ds(pos, 1), :]
        sin_b[pl.ds(b, 1), :] = sin_t[pl.ds(pos, 1), :]
        return 0
    lax.fori_loop(0, B, rope_rows, 0)

    for l in range(2):
        ids = lax.broadcasted_iota(jnp.int32, (LANES, B), 0)
        picked = jnp.zeros((LANES, B), jnp.float32)
        for k in range(8):
            picked = jnp.where(ids == choice_v[l, pl.ds(k, 1), :], 1.0, picked)
        mask_s[l] = picked.T

    lane = lax.broadcasted_iota(jnp.int32, (B, LANES), 1)
    left = lane < HEAD
    lower = (lane % HEAD) < 32

    def norm_into(src, gain_ref, l):
        for hf in range(2):
            xs = [hb[src, 4 * hf + c].astype(jnp.float32) for c in range(4)]
            sq = xs[0] * xs[0]
            for x in xs[1:]:
                sq = sq + x * x
            scale = lax.rsqrt(jnp.sum(sq, axis=-1, keepdims=True) * (1.0 / D) + EPS)
            for c in range(4):
                g = gain_ref[pl.ds(l, 1), pl.ds(COLS * c, COLS)].astype(jnp.float32)
                m_s[pl.ds(ROWS * hf, ROWS), pl.ds(COLS * c, COLS)] = (xs[c] * scale * g).astype(jnp.bfloat16)

    def rope(x):
        rot = jnp.where(lower, -pltpu.roll(x, 96, 1), pltpu.roll(x, 32, 1))
        return x * cos_b[...] + rot * sin_b[...]

    def rounded(x):
        return x.astype(jnp.bfloat16).astype(jnp.float32)

    def project(l, src):
        norm_into(src, ga, l)
        qkv = dot_nt(m_s[...], wqkv[l])
        qa = rounded(rope(qkv[:, 0:LANES]))
        kq = rounded(rope(qkv[:, LANES:TILE]))
        zero = jnp.zeros_like(qa)
        qs[pl.ds(0, B, stride=8), :] = jnp.where(left, qa, zero)
        qs[pl.ds(1, B, stride=8), :] = jnp.where(left, pltpu.roll(qa, HEAD, 1), zero)
        qs[pl.ds(2, B, stride=8), :] = jnp.where(left, pltpu.roll(kq, HEAD, 1), zero)
        kvn[...] = jnp.where(left, kq, rounded(qkv[:, TILE:COLS]))

    row_ids = lax.broadcasted_iota(jnp.int32, (SEQ, LANES), 0)
    lane8 = lax.broadcasted_iota(jnp.int32, (8, LANES), 1)

    def attend(l):
        def chunk(c, _):
            if l == 0:
                landed(recv.at[l, pl.ds(0, 2), pl.ds(0, N - 1)], a2a_rs.at[l, 2 * c])
            else:
                a2a_wait(l, 2 * c)
                a2a_wait(l, 2 * c + 1)
            tiles, scores = [], []
            for i in range(8):
                b = c * 8 + i
                pos = len_s[b]
                tile = recv[l, 2 * c + i // 4, :, i % 4].reshape(SEQ, LANES).astype(jnp.float32)
                tile = jnp.where(row_ids == pos, kvn[pl.ds(b, 1), :], tile).astype(jnp.bfloat16)
                recv[l, 2 * c + i // 4, :, i % 4] = tile.reshape(8, ROWS, LANES)
                q = qs[pl.ds(pl.multiple_of(b * 8, 8), 8), :].astype(jnp.bfloat16)
                scores.append(jnp.where(lane8 <= pos, dot_nt(q, tile) * 0.125, -1e30))
                tiles.append(tile)
            s = jnp.concatenate(scores, axis=0)
            e = jnp.exp(s - jnp.max(s, axis=-1, keepdims=True))
            p = e / jnp.sum(e, axis=-1, keepdims=True)
            for i in range(8):
                b = c * 8 + i
                o = dot_nn(p[8 * i:8 * i + 8].astype(jnp.bfloat16), tiles[i])
                os_[pl.ds(pl.multiple_of(b * 8, 8), 8), :] = o
            return 0
        lax.fori_loop(0, CH, chunk, 0)

    def attn_out(l, ar):
        o0 = os_[pl.ds(0, B, stride=8), :]
        o1 = os_[pl.ds(1, B, stride=8), :]
        o2 = os_[pl.ds(2, B, stride=8), :]
        oa = jnp.where(left, pltpu.roll(o0, HEAD, 1), o1).astype(jnp.bfloat16)
        ob = pltpu.roll(o2, HEAD, 1)[:, 0:HEAD].astype(jnp.bfloat16)
        part = dot_nn(oa, wo[l, pl.ds(0, LANES)]) + dot_nn(ob, wo[l, pl.ds(LANES, HEAD)])
        put_partial(ar, part)

    def put_partial(ar, part):
        for j in range(N):
            psend[ar, j] = part[ROWS * (j // 4):ROWS * (j // 4) + ROWS, COLS * (j % 4):COLS * (j % 4) + COLS].astype(jnp.bfloat16)

    def rs_copy(ar, d):
        t = peers[d]
        return pltpu.make_async_remote_copy(
            src_ref=psend.at[ar, t], dst_ref=rsb.at[ar, d],
            send_sem=ar_ss, recv_sem=rs_rs.at[ar],
            device_id=dev(t), device_id_type=pl.DeviceIdType.MESH)

    def ag_copy(ar, d):
        t = peers[d]
        return pltpu.make_async_remote_copy(
            src_ref=hb.at[ar + 1, me], dst_ref=hb.at[ar + 1, me],
            send_sem=ar_ss, recv_sem=ag_rs.at[ar],
            device_id=dev(t), device_id_type=pl.DeviceIdType.MESH)

    def reduce_all(ar, filler=None):
        for d in range(N - 1):
            rs_copy(ar, d).start()
        if filler is not None:
            filler()
        total = psend[ar, me].astype(jnp.float32)
        landed(rsb.at[ar], rs_rs.at[ar])
        for d in range(N - 1):
            total = total + rsb[ar, d].astype(jnp.float32)
        hb[ar + 1, me] = (hb[ar, me].astype(jnp.float32) + total).astype(jnp.bfloat16)
        for d in range(N - 1):
            ag_copy(ar, d).start()

    def gather_wait(ar):
        landed(rsb.at[ar], ag_rs.at[ar])

    out_refs = (outs1, outs2)

    def write_caches(l):
        def chunk(c, _):
            for i in range(8):
                out_refs[l][c * 8 + i] = recv[l, 2 * c + i // 4, :, i % 4].reshape(SEQ, LANES).T
            return 0
        lax.fori_loop(0, CH, chunk, 0)

    def turn(l, lo, hi):
        def quad(j, _):
            rows = weight_rows(j)
            landed(wg.at[l, pl.ds(0, SLOTS)], s_w.at[l, j])
            for w in (wg, wu):
                for k in range(6):
                    cols = pl.ds(TILE * k, TILE)
                    w[l, rows, cols] = w[l, rows, cols].T
            return 0
        lax.fori_loop(lo, hi, quad, 0)

    lane_w = lax.broadcasted_iota(jnp.int32, (B, LANES), 1) < HEAD

    def experts(l, ar):
        norm_into(ar, gm, l)

        def up(j):
            rows = weight_rows(j)
            g = u = None
            for k in range(6):
                cols = pl.ds(TILE * k, TILE)
                x = m_s[:, cols]
                dg, du = dot_nn(x, wg[l, rows, cols]), dot_nn(x, wu[l, rows, cols])
                g, u = (dg, du) if g is None else (g + dg, u + du)
            act[j] = g * jax.nn.sigmoid(g) * u

        logits = dot_nt(m_s[...], wr[l])
        up(0)
        up(1)
        chosen = mask_s[l][:, 0:40] > 0.5
        top = jnp.max(jnp.where(chosen, logits, -jnp.inf), axis=-1, keepdims=True)
        e = jnp.where(chosen, jnp.exp(jnp.where(chosen, logits - top, 0.0)), 0.0)
        gate = e / jnp.sum(e, axis=-1, keepdims=True)
        for j in range(QUADS):
            for i in range(2):
                k = 4 * j + 2 * i
                g0 = jnp.broadcast_to(gate[:, k:k + 1], (B, LANES))
                g1 = jnp.broadcast_to(gate[:, k + 1:k + 2], (B, LANES))
                gx[j, :, pl.ds(LANES * i, LANES)] = jnp.where(left, g0, g1)
        for j in range(2, QUADS):
            up(j)
        landed(wd.at[l], s_d.at[l])
        for j in range(QUADS):
            acts[:, pl.ds(TILE * j, TILE)] = (gx[j] * act[j]).astype(jnp.bfloat16)
        for half in range(2):
            part = dot_nn(acts[...], wd[l, :, pl.ds(WIDE * half, WIDE)])
            for j in range(N):
                if (j % 4) // 2 == half:
                    lo = COLS * (j % 2)
                    psend[ar, j] = part[ROWS * (j // 4):ROWS * (j // 4) + ROWS, lo:lo + COLS].astype(jnp.bfloat16)

    SC = jax.named_scope
    with SC("p_proj0"):
        project(0, 0)
    with SC("p_prep1"):
        for c in range(CH):
            prep(1, c)
        a2a_send(1, 0)
    with SC("p_turn0"):
        turn(0, 0, 10)
    with SC("p_att0"):
        attend(0)
    with SC("p_aout0"):
        attn_out(0, 0)

    def fill_rs0():
        a2a_send(1, 1)
        a2a_send(1, 2)
        write_caches(0)

    with SC("p_rs0"):
        reduce_all(0, fill_rs0)
    with SC("p_ag0"):
        a2a_send(1, 3)
        a2a_send(1, 4)
        turn(1, 0, 4)
        gather_wait(0)
    for p in range(5, TP):
        a2a_send(1, p)
    with SC("p_moe0"):
        experts(0, 1)
    with SC("p_rs1"):
        reduce_all(1, lambda: turn(1, 4, 6))
    with SC("p_ag1"):
        turn(1, 6, 8)
        gather_wait(1)
    with SC("p_proj1"):
        project(1, 2)
    with SC("p_att1"):
        attend(1)
    with SC("p_aout1"):
        attn_out(1, 2)
    with SC("p_rs2"):
        reduce_all(2, lambda: write_caches(1))
    with SC("p_ag2"):
        turn(1, 8, 10)
        gather_wait(2)
    with SC("p_moe1"):
        experts(1, 3)
    with SC("p_rs3"):
        reduce_all(3)
    with SC("p_ag3"):
        gather_wait(3)
    with SC("p_end"):
        for j in range(N):
            hid_o[pl.ds(ROWS * (j // 4), ROWS), pl.ds(COLS * (j % 4), COLS)] = hb[4, j]
        landed(send.at[:, :, pl.ds(0, N - 1)], a2a_ss)
        landed(rsb, ar_ss)
        landed(rsb, ar_ss)


def tail_kernel(hid, kv1, kv2, hid_o, k1_o, v1_o, k2_o, v2_o, sem):
    copies = [
        (kv1.at[:, pl.ds(0, HEAD)], k1_o), (kv1.at[:, pl.ds(HEAD, HEAD)], v1_o),
        (kv2.at[:, pl.ds(0, HEAD)], k2_o), (kv2.at[:, pl.ds(HEAD, HEAD)], v2_o),
        (hid, hid_o),
    ]
    cps = [pltpu.make_async_copy(src, dst, sem.at[i]) for i, (src, dst) in enumerate(copies)]
    for cp in cps:
        cp.start()
    for cp in cps:
        cp.wait()


def solution(mesh):
    seq_spec = P('dp', 'tp', None, None)
    head_spec = P('dp', None, 'tp', None)
    col_spec = P(None, None, 'tp')
    ff_spec = P(None, None, None, 'tp')
    cos, sin = rope_tables()

    def local_step(hidden, lengths, choice, keys_one, vals_one, keys_two, vals_two, g_attn, w_q, w_k, w_v, w_o, g_mlp, w_router, w_gate, w_up, w_down):
        bf, f32 = jnp.bfloat16, jnp.float32
        any_spec = pl.BlockSpec(memory_space=pl.ANY)
        vmem_spec = pl.BlockSpec(memory_space=pltpu.VMEM)
        dma = pltpu.SemaphoreType.DMA
        vm = pltpu.VMEM
        operands = (
            lengths, hidden, jnp.swapaxes(choice, 1, 2),
            keys_one.reshape(SLOTS, 8, HEAD), vals_one.reshape(SLOTS, 8, HEAD), keys_two.reshape(SLOTS, 8, HEAD), vals_two.reshape(SLOTS, 8, HEAD),
            g_attn, jnp.swapaxes(w_q, 1, 2), jnp.swapaxes(w_k, 1, 2), jnp.swapaxes(w_v, 1, 2), w_o, g_mlp, jnp.swapaxes(w_router, 1, 2),
            jnp.swapaxes(w_gate, 2, 3).reshape(2, 2560, D), jnp.swapaxes(w_up, 2, 3).reshape(2, 2560, D), w_down.reshape(2, 2560, D),
            jnp.asarray(cos), jnp.asarray(sin),
        )
        hid, kv1, kv2 = pl.pallas_call(
            kernel,
            name='decode_two',
            out_shape=[vm((B, D), bf), vm((B, LANES, LANES), bf), vm((B, LANES, LANES), bf)],
            in_specs=[pl.BlockSpec(memory_space=pltpu.SMEM)] + [any_spec] * 18,
            out_specs=[vmem_spec] * 3,
            scratch_shapes=[
                vm((2, 2560, D), bf), vm((2, 2560, D), bf), vm((2, 2560, D), bf),
                vm((2, COLS, D), bf), vm((2, 192, D), bf), vm((2, 40, D), bf),
                vm((2, SLOTS, 8, HEAD), bf), vm((2, SLOTS, 8, HEAD), bf), vm((1024, LANES), f32),
                vm((2, TP, 8, 4, ROWS, LANES), bf), vm((2, TP, 8, 4, ROWS, LANES), bf),
                vm((5, 8, ROWS, COLS), bf), vm((4, 8, ROWS, COLS), bf), vm((4, 7, ROWS, COLS), bf),
                vm((B, D), bf), vm((TILE, LANES), f32), vm((8, LANES), f32), vm((TILE, LANES), f32), vm((B, LANES), f32),
                vm((LANES, LANES), f32), vm((LANES, LANES), f32), vm((B, LANES), f32), vm((B, LANES), f32),
                vm((2, 8, B), jnp.int32), vm((2, D), bf), vm((2, D), bf),
                vm((2, B, LANES), f32), vm((QUADS, B, TILE), f32), vm((QUADS, B, TILE), f32), vm((B, 2560), bf),
                dma((2, CH)), dma((2, QUADS)), dma((2,)), dma, dma, dma((2, TP)), dma, dma((4,)), dma((4,)),
            ],
            compiler_params=pltpu.CompilerParams(collective_id=0, has_side_effects=True, vmem_limit_bytes=63500000),
        )(*operands)
        hid_out, *caches = pl.pallas_call(
            tail_kernel,
            name='write_out',
            out_shape=[jax.ShapeDtypeStruct((B, D), bf)] + [jax.ShapeDtypeStruct((B, HEAD, LANES), bf)] * 4,
            in_specs=[vmem_spec] * 3,
            out_specs=[any_spec] * 5,
            scratch_shapes=[dma((5,))],
            compiler_params=pltpu.CompilerParams(vmem_limit_bytes=4 << 20),
        )(hid, kv1, kv2)
        return (hid_out, *[jnp.swapaxes(kv, 1, 2)[:, :, None, :] for kv in caches])

    return jax.shard_map(local_step, mesh=mesh, in_specs=(P('dp', None), P('dp'), P(None, 'dp', None), seq_spec, seq_spec, seq_spec, seq_spec, P(), col_spec, col_spec, col_spec, P(None, 'tp', None), P(), P(), ff_spec, ff_spec, P(None, None, 'tp', None)), out_specs=(P('dp', None), head_spec, head_spec, head_spec, head_spec), check_vma=False)
```

time: 68.7 us -> 60.2 us (0.88)
  Pallas kernels: 68 us -> 59.4 us
    pallas_call x1, Pallas kernels: 66.6 us -> 58 us  [local_step(): pl.pallas_call(kernel, name='decode_two', out_shape=[vm((B, D), bf), vm((...]
where the time goes in v3:
time: 60.2 us; the launch traced here: 60 us
  Pallas kernels  59.4 us (99%)
  between operations  0.65 us (1%)
    pallas_call x1, Pallas kernels, local_step(): pl.pallas_call(kernel, name='decode_two', out_shape=[vm((B, D), bf), vm((...  58 us
    pallas_call x1, Pallas kernels, local_step(): pl.pallas_call(tail_kernel, name='write_out', out_shape=[jax.ShapeDtypeSt...  1.38 us

profile of v3, /device:TPU:0, one launch (start us, length us, event | category | flops | bytes accessed | tf_op | source)
XLA Modules:
  0.0 60.0 jit_solution(5610716717776314134)
XLA Ops:
  0.6 58.0 %decode_two.1 = (bf16[32,1536]{1,0:T(8,128)(2,1)S(1)}, bf16[32,128,128]{2,1,0:T(8,128)(2,1)S(1)}, bf16[32,128,128]{2,1,0:T(8,128)(2,1)S(1)}) custom-call(s32[32]{0:T(128)} %len_s.1, bf16[32,1536]{1,0:T(8,128)(2,1)} %hid_h.1, s32[2,8,32]{2,1,0:T(8,128)} %bitcast.47, bf16[512,8,64]{2,1,0:T(8,128)(2,1)} %bitcast.40, bf16[512,8,64]{2,1,0:T(8,128)(2,1)} %bitcast.41, ...), custom_call_target="tpu_custom_call" | custom-call | tf_op jit(solution)/shard_map/decode_two/pallas_call | solution.py:434
  58.7 1.4 %write_out.1 = (bf16[32,1536]{1,0:T(8,128)(2,1)}, bf16[32,64,128]{2,1,0:T(8,128)(2,1)}, bf16[32,64,128]{2,1,0:T(8,128)(2,1)}, bf16[32,64,128]{2,1,0:T(8,128)(2,1)}, bf16[32,64,128]{2,1,0:T(8,128)(2,1)}) custom-call(bf16[32,1536]{1,0:T(8,128)(2,1)S(1)} %get-tuple-element.13.hid, bf16[32,128,128]{2,1,0:T(8,128)(2,1)S(1)} %get-tuple-element.14.kv1, ...), custom_call_target="tpu_custom_call" | custom-call | tf_op jit(solution)/shard_map/write_out/pallas_call | solution.py:454

commit v4 on v3

--- a/solution.py
+++ b/solution.py
@@ -37,9 +37,9 @@
     return jnp.dot(a, b, preferred_element_type=jnp.float32)
 
 
-def kernel(len_s, hid_h, choice_h, k1_h, v1_h, k2_h, v2_h, ga_h, wq_h, wk_h, wv_h, wo_h, gm_h, wr_h, wg_h, wu_h, wd_h, cos_h, sin_h,
+def kernel(len_h, hid_h, choice_h, k1_h, v1_h, k2_h, v2_h, ga_h, wq_h, wk_h, wv_h, wo_h, gm_h, wr_h, wg_h, wu_h, wd_h, cos_h, sin_h,
            hid_o, outs1, outs2,
-           wg, wu, wd, wqkv, wo, wr, xk, xv, stage, send, recv, hb, psend, rsb, m_s, qs, sc, os_, kvn, cos_t, sin_t, cos_b, sin_b, choice_v, ga, gm, mask_s, gx, act, acts,
+           len_s, wg, wu, wd, wqkv, wo, wr, xk, xv, stage, send, recv, hb, psend, rsb, m_s, qs, sc, os_, kvn, cos_t, sin_t, cos_b, sin_b, choice_v, ga, gm, mask_s, gx, act, acts,
            s_in, s_w, s_d, s_small, a2a_ss, a2a_rs, ar_ss, rs_rs, ag_rs):
     me = lax.axis_index('tp')
     my, mx, mc = me // 4, (me // 2) % 2, me % 2
@@ -59,7 +59,7 @@
         for c in range(CH):
             for i, buf in enumerate((xk, xv)):
                 rows = pl.ds(c * LANES, LANES)
-                cp = pltpu.make_async_copy(caches[l][i].at[rows], buf.at[l, rows], s_in.at[l, c])
+                cp = pltpu.make_async_copy(caches[l][i].at[rows], buf.at[l, rows], s_in.at[c if l == 0 else CH])
                 cache_cp[l, c, i] = cp
 
     for c in range(CH):
@@ -71,7 +71,7 @@
         pl.semaphore_signal(barrier, inc=1, device_id=dev(t), device_id_type=pl.DeviceIdType.MESH)
 
     small = [
-        (cos_h, cos_t), (sin_h, sin_t), (choice_h, choice_v), (ga_h, ga), (gm_h, gm), (wr_h, wr), (wo_h, wo),
+        (len_h, len_s), (cos_h, cos_t), (sin_h, sin_t), (choice_h, choice_v), (ga_h, ga), (gm_h, gm), (wr_h, wr), (wo_h, wo),
     ]
     for l in range(2):
         small.append((wq_h.at[l, pl.ds(0, LANES)], wqkv.at[l, pl.ds(0, LANES)]))
@@ -94,8 +94,8 @@
         for l in range(2):
             def start_gate_up(j, _, l=l):
                 rows = weight_rows(j)
-                pltpu.make_async_copy(wg_h.at[l, rows], wg.at[l, rows], s_w.at[l, j]).start()
-                pltpu.make_async_copy(wu_h.at[l, rows], wu.at[l, rows], s_w.at[l, j]).start()
+                pltpu.make_async_copy(wg_h.at[l, rows], wg.at[l, rows], s_w.at[j if l == 0 else QUADS]).start()
+                pltpu.make_async_copy(wu_h.at[l, rows], wu.at[l, rows], s_w.at[j if l == 0 else QUADS]).start()
                 return 0
             lax.fori_loop(0, QUADS, start_gate_up, 0)
             def start_down(j, _, l=l):
@@ -105,7 +105,8 @@
             lax.fori_loop(0, QUADS, start_down, 0)
 
     def prep(l, c):
-        landed(xk.at[l, pl.ds(0, TILE)], s_in.at[l, c])
+        if l == 0:
+            landed(xk.at[l, pl.ds(0, TILE)], s_in.at[c])
         for i in range(2):
             rows = pl.ds(c * LANES + i * HEAD, HEAD)
             kk = xk[l, rows].astype(jnp.float32)
@@ -120,35 +121,26 @@
         t = peers[d]
         return pltpu.make_async_remote_copy(
             src_ref=send.at[l, p, t], dst_ref=recv.at[l, p, me],
-            send_sem=a2a_ss, recv_sem=a2a_rs.at[l, p],
+            send_sem=a2a_ss, recv_sem=a2a_rs.at[p // 2 if l == 0 else CH],
             device_id=dev(t), device_id_type=pl.DeviceIdType.MESH)
-
-    def a2a_send2(l, p):
-        for d in range(N - 1):
-            t = peers[d]
-            pltpu.make_async_remote_copy(
-                src_ref=send.at[l, pl.ds(p, 2), t], dst_ref=recv.at[l, pl.ds(p, 2), me],
-                send_sem=a2a_ss, recv_sem=a2a_rs.at[l, p],
-                device_id=dev(t), device_id_type=pl.DeviceIdType.MESH).start()
-        recv[l, pl.ds(p, 2), me] = send[l, pl.ds(p, 2), me]
 
     def a2a_send(l, p):
         for d in range(N - 1):
             a2a_copy(l, p, d).start()
-        recv[l, p, me] = send[l, p, me]
-
-    def a2a_wait(l, p):
-        landed(recv.at[l, p, pl.ds(0, N - 1)], a2a_rs.at[l, p])
+        if l == 0:
+            recv[l, p, me] = send[l, p, me]
 
     with jax.named_scope('p_prep0'):
         prep(0, 0)
     with jax.named_scope('p_bar'):
         pl.semaphore_wait(barrier, N - 1)
     with jax.named_scope('p_send0'):
-        a2a_send2(0, 0)
+        a2a_send(0, 0)
+        a2a_send(0, 1)
         for c in range(1, CH):
             prep(0, c)
-            a2a_send2(0, 2 * c)
+            a2a_send(0, 2 * c)
+            a2a_send(0, 2 * c + 1)
     with jax.named_scope('p_rest'):
         start_rest()
 
@@ -196,7 +188,15 @@
 
     def project(l, src):
         norm_into(src, ga, l)
-        qkv = dot_nt(m_s[...], wqkv[l])
+        if l == 0:
+            qkv = dot_nt(m_s[...], wqkv[l])
+        else:
+            qkv = None
+            for k in range(6):
+                tile = jnp.concatenate([jnp.concatenate([
+                    wqkv[l, pl.ds(LANES * a, LANES), pl.ds(LANES * i, LANES)] for i in (2 * k, 2 * k + 1)], axis=0) for a in range(3)], axis=1)
+                part = dot_nn(m_s[:, pl.ds(TILE * k, TILE)], tile)
+                qkv = part if qkv is None else qkv + part
         qa = rounded(rope(qkv[:, 0:LANES]))
         kq = rounded(rope(qkv[:, LANES:TILE]))
         zero = jnp.zeros_like(qa)
@@ -210,11 +210,7 @@
 
     def attend(l):
         def chunk(c, _):
-            if l == 0:
-                landed(recv.at[l, pl.ds(0, 2), pl.ds(0, N - 1)], a2a_rs.at[l, 2 * c])
-            else:
-                a2a_wait(l, 2 * c)
-                a2a_wait(l, 2 * c + 1)
+            landed(recv.at[l, pl.ds(0, 2), pl.ds(0, N - 1)], a2a_rs.at[c])
             tiles, scores = [], []
             for i in range(8):
                 b = c * 8 + i
@@ -235,18 +231,41 @@
             return 0
         lax.fori_loop(0, CH, chunk, 0)
 
+    def attend_all(l):
+        landed(recv.at[l, :, pl.ds(0, N - 1)], a2a_rs.at[CH])
+        for b in range(B):
+            pos = len_s[b]
+            spot = recv.at[l, b // 4, :, b % 4]
+            tile = spot[...].reshape(SEQ, LANES).astype(jnp.float32)
+            tile = jnp.where(row_ids == pos, kvn[pl.ds(b, 1), :], tile).astype(jnp.bfloat16)
+            spot[...] = tile.reshape(8, ROWS, LANES)
+            q = qs[pl.ds(b * 8, 8), :].astype(jnp.bfloat16)
+            sc[pl.ds(b * 8, 8), :] = jnp.where(lane8 <= pos, dot_nt(q, tile) * 0.125, -1e30)
+        s = sc[...]
+        e = jnp.exp(s - jnp.max(s, axis=-1, keepdims=True))
+        sc[...] = e / jnp.sum(e, axis=-1, keepdims=True)
+        for b in range(B):
+            p = sc[pl.ds(b * 8, 8), :].astype(jnp.bfloat16)
+            os_[pl.ds(b * 8, 8), :] = dot_nn(p, recv[l, b // 4, :, b % 4].reshape(SEQ, LANES))
+
     def attn_out(l, ar):
         o0 = os_[pl.ds(0, B, stride=8), :]
         o1 = os_[pl.ds(1, B, stride=8), :]
         o2 = os_[pl.ds(2, B, stride=8), :]
         oa = jnp.where(left, pltpu.roll(o0, HEAD, 1), o1).astype(jnp.bfloat16)
         ob = pltpu.roll(o2, HEAD, 1)[:, 0:HEAD].astype(jnp.bfloat16)
-        part = dot_nn(oa, wo[l, pl.ds(0, LANES)]) + dot_nn(ob, wo[l, pl.ds(LANES, HEAD)])
-        put_partial(ar, part)
-
-    def put_partial(ar, part):
-        for j in range(N):
-            psend[ar, j] = part[ROWS * (j // 4):ROWS * (j // 4) + ROWS, COLS * (j % 4):COLS * (j % 4) + COLS].astype(jnp.bfloat16)
+        send_halves(ar, lambda cols: dot_nn(oa, wo[l, pl.ds(0, LANES), cols]) + dot_nn(ob, wo[l, pl.ds(LANES, HEAD), cols]))
+
+    def send_halves(ar, columns):
+        for dx in (1, 0):
+            xs = (mx + dx) % 2
+            part = columns(pl.ds(pl.multiple_of(WIDE * xs, LANES), WIDE))
+            for hy in range(2):
+                for c in range(2):
+                    psend[ar, 4 * hy + 2 * xs + c] = part[ROWS * hy:ROWS * hy + ROWS, COLS * c:COLS * c + COLS].astype(jnp.bfloat16)
+            for d in range(N - 1):
+                if PEERS[d][1] == dx:
+                    rs_copy(ar, d).start()
 
     def rs_copy(ar, d):
         t = peers[d]
@@ -263,8 +282,6 @@
             device_id=dev(t), device_id_type=pl.DeviceIdType.MESH)
 
     def reduce_all(ar, filler=None):
-        for d in range(N - 1):
-            rs_copy(ar, d).start()
         if filler is not None:
             filler()
         total = psend[ar, me].astype(jnp.float32)
@@ -290,7 +307,8 @@
     def turn(l, lo, hi):
         def quad(j, _):
             rows = weight_rows(j)
-            landed(wg.at[l, pl.ds(0, SLOTS)], s_w.at[l, j])
+            if l == 0:
+                landed(wg.at[l, pl.ds(0, SLOTS)], s_w.at[j])
             for w in (wg, wu):
                 for k in range(6):
                     cols = pl.ds(TILE * k, TILE)
@@ -298,9 +316,15 @@
             return 0
         lax.fori_loop(lo, hi, quad, 0)
 
+    def turn_projection(l):
+        for a in range(3):
+            for i in range(12):
+                spot = wqkv.at[l, pl.ds(LANES * a, LANES), pl.ds(LANES * i, LANES)]
+                spot[...] = spot[...].T
+
     lane_w = lax.broadcasted_iota(jnp.int32, (B, LANES), 1) < HEAD
 
-    def experts(l, ar):
+    def experts(l, ar, pieces=()):
         norm_into(ar, gm, l)
 
         def up(j):
@@ -314,6 +338,8 @@
             act[j] = g * jax.nn.sigmoid(g) * u
 
         logits = dot_nt(m_s[...], wr[l])
+        for p in pieces:
+            a2a_send(1, p)
         up(0)
         up(1)
         chosen = mask_s[l][:, 0:40] > 0.5
@@ -331,21 +357,18 @@
         landed(wd.at[l], s_d.at[l])
         for j in range(QUADS):
             acts[:, pl.ds(TILE * j, TILE)] = (gx[j] * act[j]).astype(jnp.bfloat16)
-        for half in range(2):
-            part = dot_nn(acts[...], wd[l, :, pl.ds(WIDE * half, WIDE)])
-            for j in range(N):
-                if (j % 4) // 2 == half:
-                    lo = COLS * (j % 2)
-                    psend[ar, j] = part[ROWS * (j // 4):ROWS * (j // 4) + ROWS, lo:lo + COLS].astype(jnp.bfloat16)
+        send_halves(ar, lambda cols: dot_nn(acts[...], wd[l, :, cols]))
 
     SC = jax.named_scope
     with SC("p_proj0"):
         project(0, 0)
     with SC("p_prep1"):
+        landed(xk, s_in.at[CH])
         for c in range(CH):
             prep(1, c)
-        a2a_send(1, 0)
+        recv[1, :, me] = send[1, :, me]
     with SC("p_turn0"):
+        turn_projection(1)
         turn(0, 0, 10)
     with SC("p_att0"):
         attend(0)
@@ -353,30 +376,32 @@
         attn_out(0, 0)
 
     def fill_rs0():
+        a2a_send(1, 0)
         a2a_send(1, 1)
-        a2a_send(1, 2)
         write_caches(0)
 
     with SC("p_rs0"):
         reduce_all(0, fill_rs0)
     with SC("p_ag0"):
+        a2a_send(1, 2)
         a2a_send(1, 3)
-        a2a_send(1, 4)
+        landed(wg, s_w.at[QUADS])
         turn(1, 0, 4)
         gather_wait(0)
-    for p in range(5, TP):
+    for p in range(4, 7):
         a2a_send(1, p)
     with SC("p_moe0"):
         experts(0, 1)
     with SC("p_rs1"):
         reduce_all(1, lambda: turn(1, 4, 6))
     with SC("p_ag1"):
+        a2a_send(1, 7)
         turn(1, 6, 8)
         gather_wait(1)
     with SC("p_proj1"):
         project(1, 2)
     with SC("p_att1"):
-        attend(1)
+        attend_all(1)
     with SC("p_aout1"):
         attn_out(1, 2)
     with SC("p_rs2"):
@@ -435,19 +460,20 @@
             kernel,
             name='decode_two',
             out_shape=[vm((B, D), bf), vm((B, LANES, LANES), bf), vm((B, LANES, LANES), bf)],
-            in_specs=[pl.BlockSpec(memory_space=pltpu.SMEM)] + [any_spec] * 18,
+            in_specs=[any_spec] * 19,
             out_specs=[vmem_spec] * 3,
             scratch_shapes=[
+                pltpu.SMEM((B,), jnp.int32),
                 vm((2, 2560, D), bf), vm((2, 2560, D), bf), vm((2, 2560, D), bf),
                 vm((2, COLS, D), bf), vm((2, 192, D), bf), vm((2, 40, D), bf),
                 vm((2, SLOTS, 8, HEAD), bf), vm((2, SLOTS, 8, HEAD), bf), vm((1024, LANES), f32),
                 vm((2, TP, 8, 4, ROWS, LANES), bf), vm((2, TP, 8, 4, ROWS, LANES), bf),
                 vm((5, 8, ROWS, COLS), bf), vm((4, 8, ROWS, COLS), bf), vm((4, 7, ROWS, COLS), bf),
-                vm((B, D), bf), vm((TILE, LANES), f32), vm((8, LANES), f32), vm((TILE, LANES), f32), vm((B, LANES), f32),
+                vm((B, D), bf), vm((TILE, LANES), f32), vm((TILE, LANES), f32), vm((TILE, LANES), f32), vm((B, LANES), f32),
                 vm((LANES, LANES), f32), vm((LANES, LANES), f32), vm((B, LANES), f32), vm((B, LANES), f32),
                 vm((2, 8, B), jnp.int32), vm((2, D), bf), vm((2, D), bf),
                 vm((2, B, LANES), f32), vm((QUADS, B, TILE), f32), vm((QUADS, B, TILE), f32), vm((B, 2560), bf),
-                dma((2, CH)), dma((2, QUADS)), dma((2,)), dma, dma, dma((2, TP)), dma, dma((4,)), dma((4,)),
+                dma((CH + 1,)), dma((QUADS + 1,)), dma((2,)), dma, dma, dma((CH + 1,)), dma, dma((4,)), dma((4,)),
             ],
             compiler_params=pltpu.CompilerParams(collective_id=0, has_side_effects=True, vmem_limit_bytes=63500000),
         )(*operands)

time: 60.2 us -> 58.1 us (0.965)
  Pallas kernels: 59.4 us -> 57.3 us
    pallas_call x1, Pallas kernels: 58 us -> 55.9 us  [local_step(): pl.pallas_call(kernel, name='decode_two', out_shape=[vm((B, D), bf), vm((...]
where the time goes in v4:
time: 58.1 us; the launch traced here: 58 us
  Pallas kernels  57.3 us (99%)
  between operations  0.65 us (1%)
    pallas_call x1, Pallas kernels, local_step(): pl.pallas_call(kernel, name='decode_two', out_shape=[vm((B, D), bf), vm((...  55.9 us
    pallas_call x1, Pallas kernels, local_step(): pl.pallas_call(tail_kernel, name='write_out', out_shape=[jax.ShapeDtypeSt...  1.38 us

profile of v4, /device:TPU:0, one launch (start us, length us, event | category | flops | bytes accessed | tf_op | source)
XLA Modules:
  0.0 58.0 jit_solution(11285246371227368199)
XLA Ops:
  0.6 55.9 %decode_two.1 = (bf16[32,1536]{1,0:T(8,128)(2,1)S(1)}, bf16[32,128,128]{2,1,0:T(8,128)(2,1)S(1)}, bf16[32,128,128]{2,1,0:T(8,128)(2,1)S(1)}) custom-call(s32[32]{0:T(128)} %len_h.1, bf16[32,1536]{1,0:T(8,128)(2,1)} %hid_h.1, s32[2,8,32]{2,1,0:T(8,128)} %bitcast.47, bf16[512,8,64]{2,1,0:T(8,128)(2,1)} %bitcast.40, bf16[512,8,64]{2,1,0:T(8,128)(2,1)} %bitcast.41, ...), custom_call_target="tpu_custom_call" | custom-call | tf_op jit(solution)/shard_map/decode_two/pallas_call | solution.py:459
  56.6 1.4 %write_out.1 = (bf16[32,1536]{1,0:T(8,128)(2,1)}, bf16[32,64,128]{2,1,0:T(8,128)(2,1)}, bf16[32,64,128]{2,1,0:T(8,128)(2,1)}, bf16[32,64,128]{2,1,0:T(8,128)(2,1)}, bf16[32,64,128]{2,1,0:T(8,128)(2,1)}) custom-call(bf16[32,1536]{1,0:T(8,128)(2,1)S(1)} %get-tuple-element.13.hid, bf16[32,128,128]{2,1,0:T(8,128)(2,1)S(1)} %get-tuple-element.14.kv1, ...), custom_call_target="tpu_custom_call" | custom-call | tf_op jit(solution)/shard_map/write_out/pallas_call | solution.py:480

commit v5 on v4

--- a/solution.py
+++ b/solution.py
@@ -39,7 +39,7 @@
 
 def kernel(len_h, hid_h, choice_h, k1_h, v1_h, k2_h, v2_h, ga_h, wq_h, wk_h, wv_h, wo_h, gm_h, wr_h, wg_h, wu_h, wd_h, cos_h, sin_h,
            hid_o, outs1, outs2,
-           len_s, wg, wu, wd, wqkv, wo, wr, xk, xv, stage, send, recv, hb, psend, rsb, m_s, qs, sc, os_, kvn, cos_t, sin_t, cos_b, sin_b, choice_v, ga, gm, mask_s, gx, act, acts,
+           len_s, wg, wu, wd, wqkv, wo, wr, xk, xv, stage, send, recv, hb, psend, rsb, m_s, qs, os_, kvn, cos_t, sin_t, cos_b, sin_b, choice_v, ga, gm, mask_s, gx, act, acts,
            s_in, s_w, s_d, s_small, a2a_ss, a2a_rs, ar_ss, rs_rs, ag_rs):
     me = lax.axis_index('tp')
     my, mx, mc = me // 4, (me // 2) % 2, me % 2
@@ -94,8 +94,8 @@
         for l in range(2):
             def start_gate_up(j, _, l=l):
                 rows = weight_rows(j)
-                pltpu.make_async_copy(wg_h.at[l, rows], wg.at[l, rows], s_w.at[j if l == 0 else QUADS]).start()
-                pltpu.make_async_copy(wu_h.at[l, rows], wu.at[l, rows], s_w.at[j if l == 0 else QUADS]).start()
+                pltpu.make_async_copy(wg_h.at[l, rows], wg.at[l, rows], s_w.at[l]).start()
+                pltpu.make_async_copy(wu_h.at[l, rows], wu.at[l, rows], s_w.at[l]).start()
                 return 0
             lax.fori_loop(0, QUADS, start_gate_up, 0)
             def start_down(j, _, l=l):
@@ -240,12 +240,12 @@
             tile = jnp.where(row_ids == pos, kvn[pl.ds(b, 1), :], tile).astype(jnp.bfloat16)
             spot[...] = tile.reshape(8, ROWS, LANES)
             q = qs[pl.ds(b * 8, 8), :].astype(jnp.bfloat16)
-            sc[pl.ds(b * 8, 8), :] = jnp.where(lane8 <= pos, dot_nt(q, tile) * 0.125, -1e30)
-        s = sc[...]
+            os_[pl.ds(b * 8, 8), :] = jnp.where(lane8 <= pos, dot_nt(q, tile) * 0.125, -1e30)
+        s = os_[...]
         e = jnp.exp(s - jnp.max(s, axis=-1, keepdims=True))
-        sc[...] = e / jnp.sum(e, axis=-1, keepdims=True)
+        os_[...] = e / jnp.sum(e, axis=-1, keepdims=True)
         for b in range(B):
-            p = sc[pl.ds(b * 8, 8), :].astype(jnp.bfloat16)
+            p = os_[pl.ds(b * 8, 8), :].astype(jnp.bfloat16)
             os_[pl.ds(b * 8, 8), :] = dot_nn(p, recv[l, b // 4, :, b % 4].reshape(SEQ, LANES))
 
     def attn_out(l, ar):
@@ -307,8 +307,6 @@
     def turn(l, lo, hi):
         def quad(j, _):
             rows = weight_rows(j)
-            if l == 0:
-                landed(wg.at[l, pl.ds(0, SLOTS)], s_w.at[j])
             for w in (wg, wu):
                 for k in range(6):
                     cols = pl.ds(TILE * k, TILE)
@@ -369,6 +367,7 @@
         recv[1, :, me] = send[1, :, me]
     with SC("p_turn0"):
         turn_projection(1)
+        landed(wg, s_w.at[0])
         turn(0, 0, 10)
     with SC("p_att0"):
         attend(0)
@@ -385,7 +384,7 @@
     with SC("p_ag0"):
         a2a_send(1, 2)
         a2a_send(1, 3)
-        landed(wg, s_w.at[QUADS])
+        landed(wg, s_w.at[1])
         turn(1, 0, 4)
         gather_wait(0)
     for p in range(4, 7):
@@ -469,11 +468,11 @@
                 vm((2, SLOTS, 8, HEAD), bf), vm((2, SLOTS, 8, HEAD), bf), vm((1024, LANES), f32),
                 vm((2, TP, 8, 4, ROWS, LANES), bf), vm((2, TP, 8, 4, ROWS, LANES), bf),
                 vm((5, 8, ROWS, COLS), bf), vm((4, 8, ROWS, COLS), bf), vm((4, 7, ROWS, COLS), bf),
-                vm((B, D), bf), vm((TILE, LANES), f32), vm((TILE, LANES), f32), vm((TILE, LANES), f32), vm((B, LANES), f32),
+                vm((B, D), bf), vm((TILE, LANES), f32), vm((TILE, LANES), f32), vm((B, LANES), f32),
                 vm((LANES, LANES), f32), vm((LANES, LANES), f32), vm((B, LANES), f32), vm((B, LANES), f32),
                 vm((2, 8, B), jnp.int32), vm((2, D), bf), vm((2, D), bf),
                 vm((2, B, LANES), f32), vm((QUADS, B, TILE), f32), vm((QUADS, B, TILE), f32), vm((B, 2560), bf),
-                dma((CH + 1,)), dma((QUADS + 1,)), dma((2,)), dma, dma, dma((CH + 1,)), dma, dma((4,)), dma((4,)),
+                dma((CH + 1,)), dma((2,)), dma((2,)), dma, dma, dma((CH + 1,)), dma, dma((4,)), dma((4,)),
             ],
             compiler_params=pltpu.CompilerParams(collective_id=0, has_side_effects=True, vmem_limit_bytes=63500000),
         )(*operands)

time: 58.1 us -> 59.1 us (1.017)
  Pallas kernels: 57.3 us -> 58.3 us
    pallas_call x1, Pallas kernels: 55.9 us -> 57 us  [local_step(): pl.pallas_call(kernel, name='decode_two', out_shape=[vm((B, D), bf), vm((...]
where the time goes in v5:
time: 59.1 us; the launch traced here: 59 us
  Pallas kernels  58.3 us (99%)
  between operations  0.65 us (1%)
    pallas_call x1, Pallas kernels, local_step(): pl.pallas_call(kernel, name='decode_two', out_shape=[vm((B, D), bf), vm((...  57 us
    pallas_call x1, Pallas kernels, local_step(): pl.pallas_call(tail_kernel, name='write_out', out_shape=[jax.ShapeDtypeSt...  1.38 us

profile of v5, /device:TPU:0, one launch (start us, length us, event | category | flops | bytes accessed | tf_op | source)
XLA Modules:
  0.0 59.0 jit_solution(3237567570424135384)
XLA Ops:
  0.6 57.0 %decode_two.1 = (bf16[32,1536]{1,0:T(8,128)(2,1)S(1)}, bf16[32,128,128]{2,1,0:T(8,128)(2,1)S(1)}, bf16[32,128,128]{2,1,0:T(8,128)(2,1)S(1)}) custom-call(s32[32]{0:T(128)} %len_h.1, bf16[32,1536]{1,0:T(8,128)(2,1)} %hid_h.1, s32[2,8,32]{2,1,0:T(8,128)} %bitcast.47, bf16[512,8,64]{2,1,0:T(8,128)(2,1)} %bitcast.40, bf16[512,8,64]{2,1,0:T(8,128)(2,1)} %bitcast.41, ...), custom_call_target="tpu_custom_call" | custom-call | tf_op jit(solution)/shard_map/decode_two/pallas_call | solution.py:458
  57.6 1.4 %write_out.1 = (bf16[32,1536]{1,0:T(8,128)(2,1)}, bf16[32,64,128]{2,1,0:T(8,128)(2,1)}, bf16[32,64,128]{2,1,0:T(8,128)(2,1)}, bf16[32,64,128]{2,1,0:T(8,128)(2,1)}, bf16[32,64,128]{2,1,0:T(8,128)(2,1)}) custom-call(bf16[32,1536]{1,0:T(8,128)(2,1)S(1)} %get-tuple-element.13.hid, bf16[32,128,128]{2,1,0:T(8,128)(2,1)S(1)} %get-tuple-element.14.kv1, ...), custom_call_target="tpu_custom_call" | custom-call | tf_op jit(solution)/shard_map/write_out/pallas_call | solution.py:479
